TPU v7x, 256 devices: a whole 4x4x8 slice. The times are simulated.
256 devices in a mesh: dp: 64 (over z_lo, x, y), tensor: 4 (over z_hi, core).
Axes of the slice: x: 4, y: 4, z: 8 (z_hi: 2, z_lo: 4; z = z_hi * 4 + z_lo), core: 2. Of those that a mesh axis runs over, the one named last changes fastest.
Arguments:
- hidden_states: float32 [32768, 2048], P(('dp', 'tensor')), may hold values from -40 to 40
- lengths: int32 [64], P('dp'), may hold values from 128 to 512
- shard_order: int32 [64], replicated, may hold values from 0 to 63, each once
- gain_attn: float32 [2048], replicated, may hold values from 0.25 to 1.75
- w_query: bfloat16 [2048, 2048], P('dp', 'tensor'), may hold values from -0.015625 to 0.015625
- w_key: bfloat16 [2048, 2048], P('dp', 'tensor'), may hold values from -0.125 to 0.125
- w_value: bfloat16 [2048, 2048], P('dp', 'tensor'), may hold values from -0.125 to 0.125
- w_out: bfloat16 [2048, 2048], P('tensor', 'dp'), may hold values from -1 to 1
- rel_bias: float32 [32, 32], P(None, 'tensor'), may hold values from -6 to 300
- gain_ff: float32 [2048], replicated, may hold values from 0.25 to 1.75
- w_gate: bfloat16 [2048, 5120], P('dp', 'tensor'), may hold values from -0.125 to 0.125
- w_up: bfloat16 [2048, 5120], P('dp', 'tensor'), may hold values from -0.125 to 0.125
- w_down: bfloat16 [5120, 2048], P('tensor', 'dp'), may hold values from -0.078125 to 0.078125
- gain_final: float32 [2048], replicated, may hold values from 0.25 to 1.75
- w_reward: float32 [2048], replicated, may hold values from -0.125 to 0.125
Outputs:
- layer_output: float32 [32768, 2048], P(('dp', 'tensor'))
- normalized_rewards: float32 [64], P('dp')
Inputs may be any that keep to these rules, and one draw needn't show every extreme that they name: `shard_order`: each of 0 to 64 - 1 appears once. `lengths`: positions at or beyond a rollout's length are padding.
All inputs are finite; a program needn't handle non-finite values.
Results may differ from a plain program's by a relative error of at most 0.02.
Values may be sent and summed in bfloat16 or wider, within the bound.
A program may use at most 128 MiB of HBM per device.

v0:
```python
import jax
import jax.numpy as jnp
from jax import lax
from jax.sharding import PartitionSpec as P

DK = 64
LEN = 512


bucket_edges = (12, 16, 23, 32, 46, 64, 91)


def in_order(parts, dim):
    parts = jnp.moveaxis(parts, 0, dim)
    shape = parts.shape
    return parts.reshape(*shape[:dim], shape[dim] * shape[dim + 1], *shape[dim + 2 :])


def from_everyone(array, axis):
    peers = lax.axis_size(axis)
    return lax.all_to_all(
        jnp.broadcast_to(array[None], (peers, *array.shape)), axis, 0, 0, tiled=True
    )


def gather_directly(array, axis, dim):
    return in_order(from_everyone(array, axis), dim)


def in_one_piece(arrays, axis, dim, along):
    ends, at = ([], 0)
    for a in arrays[:-1]:
        at += a.shape[along]
        ends.append(at)
    both = jnp.concatenate(arrays, axis=along)
    return tuple(jnp.split(lax.all_gather(both, axis, axis=dim, tiled=True), ends, axis=along))


def cut_along(array, dim, peers):
    shape = array.shape
    parts = array.reshape(*shape[:dim], peers, shape[dim] // peers, *shape[dim + 1 :])
    return jnp.moveaxis(parts, dim, 0)


def sent_and_summed(array, axis, dim):
    peers = lax.axis_size(axis)
    parts = lax.all_to_all(cut_along(array, dim, peers), axis, 0, 0, tiled=True)
    return jnp.sum(parts.astype(jnp.float32), axis=0)


def of_everyone(array, axis):
    return from_everyone(array, axis).sum(axis=0)


def packed_total(arrays, axis):
    line, at, gathered = (jnp.concatenate([a.reshape(-1) for a in arrays]), 0, [])
    running = of_everyone(line, axis)
    for a in arrays:
        gathered.append(running[at : at + a.size].reshape(a.shape))
        at += a.size
    return tuple(gathered)


def bucket_index(relative):
    distance = jnp.abs(relative)
    bucket_low = jnp.minimum(distance, 8)
    for threshold in bucket_edges:
        bucket_low = bucket_low + (distance >= threshold).astype(jnp.int32)
    return jnp.where(relative > 0, 16, 0) + bucket_low


def rms_norm(values_in, weight_gain):
    return (
        values_in
        * lax.rsqrt(jnp.mean(values_in * values_in, axis=-1, keepdims=True) + 1e-06)
        * weight_gain
    )


def reorder_blocks(values_in, ordering):
    full_shape = values_in.shape
    blocks = values_in.reshape(
        full_shape[:-1] + (ordering.shape[0], full_shape[-1] // ordering.shape[0])
    )
    return jnp.take(blocks, ordering, axis=-2).reshape(full_shape)


def local(
    hidden_states,
    lengths,
    shard_order,
    gain_attn,
    w_query,
    w_key,
    w_value,
    w_out,
    rel_bias,
    gain_ff,
    w_gate,
    w_up,
    w_down,
    gain_final,
    w_reward,
):
    groups = shard_order.shape[0]
    block_ids = jnp.arange(groups, dtype=jnp.int32)
    inverse = jnp.sum(
        block_ids[:, None] * (shard_order[:, None] == block_ids[None, :]).astype(jnp.int32), axis=0
    )
    own_rows = reorder_blocks(hidden_states, shard_order)
    attn_gain = reorder_blocks(gain_attn, shard_order)
    feed_gain = reorder_blocks(gain_ff, shard_order)
    final_gain = reorder_blocks(gain_final, shard_order)
    reward_head = reorder_blocks(w_reward, shard_order)
    row_count = own_rows.shape[0]
    row_start = lax.axis_index("tensor") * row_count
    normed = gather_directly(rms_norm(own_rows, attn_gain).astype(jnp.bfloat16), "tensor", 0)

    def contract_with(source):

        def contract(running, portion, offset):
            return jnp.dot(source, portion, preferred_element_type=jnp.float32)

        return contract

    inner_width = w_query.shape[1]
    zero_block = jnp.zeros((LEN, inner_width), jnp.float32)
    attn_contract = contract_with(normed)
    running = (zero_block, zero_block, zero_block)
    portion = in_one_piece((w_query, w_key, w_value), "dp", 0, 1)
    offset = jnp.int32(0)
    queries = attn_contract(running[0], portion[0], offset)
    key_states = attn_contract(running[1], portion[1], offset)
    value_states = attn_contract(running[2], portion[2], offset)
    head_count = inner_width // DK
    query_heads = queries.astype(jnp.bfloat16).reshape(LEN, head_count, DK).transpose(1, 0, 2)
    key_heads = key_states.astype(jnp.bfloat16).reshape(LEN, head_count, DK).transpose(1, 0, 2)
    value_heads = value_states.astype(jnp.bfloat16).reshape(LEN, head_count, DK).transpose(1, 0, 2)
    span = 2 * LEN - 1
    offsets = jnp.arange(span, dtype=jnp.int32)
    relative = jnp.where(offsets < LEN, offsets, offsets - span)
    bucket_ids = bucket_index(relative)
    onehot = (
        bucket_ids[:, None] == jnp.arange(rel_bias.shape[0], dtype=jnp.int32)[None, :]
    ).astype(jnp.float32)
    offset_bias = jnp.dot(onehot, rel_bias, precision=lax.Precision.HIGHEST).T
    length = lengths[0]
    in_range = jnp.arange(LEN, dtype=jnp.int32) < length

    def head_step(operands):
        head_query, head_key, head_value, head_offsets = operands
        repeated = jnp.tile(head_offsets, LEN)[: LEN * (span - 1)].reshape(LEN, span - 1)[:, :LEN]
        scores = jnp.dot(head_query, head_key.T, preferred_element_type=jnp.float32) + repeated
        scores = jnp.where(in_range[None, :], scores, -1e30)
        row_max = jnp.max(scores, axis=-1, keepdims=True)
        exp_scores = jnp.exp(scores - row_max)
        soft_weights = (exp_scores / jnp.sum(exp_scores, axis=-1, keepdims=True)).astype(
            jnp.bfloat16
        )
        return jnp.dot(soft_weights, head_value, preferred_element_type=jnp.float32).astype(
            jnp.bfloat16
        )

    context = lax.map(head_step, (query_heads, key_heads, value_heads, offset_bias))
    context = context.transpose(1, 0, 2).reshape(LEN, inner_width)
    attn_partial = jnp.dot(
        context, lax.all_gather(w_out, "dp", axis=1, tiled=True), preferred_element_type=jnp.float32
    ).astype(jnp.bfloat16)
    mid_own = own_rows + sent_and_summed(attn_partial, "tensor", 0)
    mid_normed = gather_directly(rms_norm(mid_own, feed_gain).astype(jnp.bfloat16), "tensor", 0)
    hidden_width = w_gate.shape[1]
    zero_hidden = jnp.zeros((LEN, hidden_width), jnp.float32)
    feed_contract = contract_with(mid_normed)
    running = (zero_hidden, zero_hidden)
    portion = in_one_piece((w_gate, w_up), "dp", 0, 1)
    offset = jnp.int32(0)
    gate_proj = feed_contract(running[0], portion[0], offset)
    up_proj = feed_contract(running[1], portion[1], offset)
    activated = (jax.nn.gelu(gate_proj, approximate=True) * up_proj).astype(jnp.bfloat16)
    feed_partial = jnp.dot(
        activated,
        lax.all_gather(w_down, "dp", axis=1, tiled=True),
        preferred_element_type=jnp.float32,
    ).astype(jnp.bfloat16)
    output_rows = mid_own + lax.psum_scatter(
        feed_partial, "tensor", scatter_dimension=0, tiled=True
    ).astype(jnp.float32)
    final_normed = rms_norm(output_rows, final_gain)
    token_score = jnp.dot(final_normed, reward_head, precision=lax.Precision.HIGHEST)
    positions = row_start + jnp.arange(row_count, dtype=jnp.int32)
    local_pool = jnp.sum(jnp.where(positions < length, token_score, 0.0))
    pooled_sum = of_everyone(local_pool, "tensor")
    reward = jnp.reshape(pooled_sum / length.astype(jnp.float32), (1,))
    rollouts = lax.axis_size("dp") * lengths.shape[0]
    first_moment, second_moment = packed_total((jnp.sum(reward), jnp.sum(reward * reward)), "dp")
    reward_mean = first_moment / rollouts
    reward_var = second_moment / rollouts - reward_mean * reward_mean
    normalized = (reward - reward_mean) / jnp.sqrt(reward_var + 1e-06)
    return (reorder_blocks(output_rows, inverse), normalized)


def solution(mesh):
    placed = (
        P(("dp", "tensor"), None),
        P("dp"),
        P(),
        P(),
        P("dp", "tensor"),
        P("dp", "tensor"),
        P("dp", "tensor"),
        P("tensor", "dp"),
        P(None, "tensor"),
        P(),
        P("dp", "tensor"),
        P("dp", "tensor"),
        P("tensor", "dp"),
        P(),
        P(),
    )
    return jax.shard_map(
        local,
        mesh=mesh,
        in_specs=placed,
        out_specs=(P(("dp", "tensor"), None), P("dp")),
        check_vma=False,
    )
```

profile of v0, /device:TPU:1, one launch (start us, length us, event | category | flops | bytes accessed | tf_op | source)
XLA Modules:
  0.0 1598.2 jit_solution(13214527331848942773)
XLA Ops:
  21.1 9.9 all-to-all-start
  32.1 48.3 %all-to-all-done = bf16[4,128,2048]{2,1,0:T(8,128)(2,1)S(1)} async-done(((bf16[4,128,2048]{2,1,0:T(8,128)(2,1)}), bf16[4,128,2048]{2,1,0:T(8,128)(2,1)S(1)}, u32[]{:S(2)}, u32[]{:S(2)}) %all-to-all-start) | async-done | bytes 2097184 | tf_op jit(solution)/shard_map/all_to_all | solution.py:21
  80.4 256.9 %all-gather.5.cloned.1.call-done = bf16[2048,1536]{1,0:T(8,128)(2,1)} async-done(((bf16[32,1536]{1,0:T(8,128)(2,1)}), bf16[2048,1536]{1,0:T(8,128)(2,1)}) %all-gather.5.cloned.1.call-update) | async-done | bytes 6291472 | tf_op jit(solution)/shard_map/all_gather | solution.py:36
  337.3 3.7 fusion.39
  343.3 3.7 fusion.42
  349.5 3.7 fusion.45
  355.7 103.8 %while.11 = (s32[]{:T(128)}, bf16[8,512,64]{1,2,0:T(8,128)(2,1)}, bf16[8,512,64]{2,1,0:T(8,128)(2,1)}, bf16[8,512,64]{2,1,0:T(8,128)(2,1)}, f32[8,1023]{1,0:T(8,...) while((s32[]{:T(128)}, bf16[8,512,64]{1,2,0:T(8,128)(2,1)}, ...), condition=%wide.region_4.7_spmd.clone, body=%wide.region_1.6_spmd.clone.sunk | while | flops 69238272 | bytes 26672264 | solution.py:164
  360.2 2.9 reshape.327
  399.1 2.9 reshape.327
  412.1 2.9 reshape.327
  459.5 227.3 %all-gather.7.cloned.1.call-done = bf16[512,2048]{0,1:T(8,128)(2,1)} async-done(((bf16[512,32]{0,1:T(8,128)(2,1)}), bf16[512,2048]{0,1:T(8,128)(2,1)}) %all-gather.7.cloned.1.call-update) | async-done | bytes 2097168 | tf_op jit(solution)/shard_map/all_gather | solution.py:167
  686.8 4.4 convolution_convert_fusion.2
  691.2 86.6 %all-to-all-start.1 = ((bf16[4,128,2048]{2,1,0:T(8,128)(2,1)}), bf16[4,128,2048]{2,1,0:T(8,128)(2,1)}, u32[]{:S(2)}, u32[]{:S(2)}) async-start(bf16[4,128,2048]{2,1,0:T(8,128)(2,1)} %bitcast.15), calls=%async_computation.1 | async-start | bytes 4194304 | tf_op jit(solution)/shard_map/all_to_all | solution.py:47
  779.2 36.7 %all-to-all-done.1 = bf16[4,128,2048]{2,1,0:T(8,128)(2,1)} async-done(((bf16[4,128,2048]{2,1,0:T(8,128)(2,1)}), bf16[4,128,2048]{2,1,0:T(8,128)(2,1)}, u32[]{:S(2)}, u32[]{:S(2)}) %all-to-all-start.1) | async-done | bytes 2097184 | tf_op jit(solution)/shard_map/all_to_all | solution.py:47
  820.1 44.2 %all_to_all.27 = bf16[4,128,2048]{2,1,0:T(8,128)(2,1)} all-to-all(bf16[4,128,2048]{2,1,0:T(8,128)(2,1)S(1)} %broadcast_in_dim.85), channel_id=1, replica_groups=mesh['dp'=64,'tensor'=4] {'tensor'}, dimensions={0} | all-to-all | bytes 4194304 | tf_op jit(solution)/shard_map/all_to_all | solution.py:21
  864.3 226.1 %all-gather.9.cloned.1.call-done = bf16[2048,2560]{1,0:T(8,128)(2,1)} async-done(((bf16[32,2560]{1,0:T(8,128)(2,1)}), bf16[2048,2560]{1,0:T(8,128)(2,1)}) %all-gather.9.cloned.1.call-update) | async-done | bytes 10485776 | tf_op jit(solution)/shard_map/all_gather | solution.py:36
  1090.4 7.8 fusion.30
  1098.2 342.1 %all-gather.11.cloned.1.call-done = bf16[1280,2048]{0,1:T(8,128)(2,1)} async-done(((bf16[1280,32]{0,1:T(8,128)(2,1)}), bf16[1280,2048]{0,1:T(8,128)(2,1)}) %all-gather.11.cloned.1.call-update) | async-done | bytes 5242896 | tf_op jit(solution)/shard_map/all_gather | solution.py:182
  1440.3 13.1 convolution_convert_fusion.1
  1454.4 98.7 %reduce-scatter.2.cloned.1.call-done = bf16[128,2048]{1,0:T(8,128)(2,1)} async-done(((bf16[512,2048]{1,0:T(8,128)(2,1)}), bf16[128,2048]{1,0:T(8,128)(2,1)}) %reduce-scatter.2.cloned.1.call-update) | async-done | bytes 524304 | tf_op jit(solution)/shard_map/reduce_scatter | solution.py:185
  1557.7 4.0 all-to-all-start.3
  1562.4 6.3 all-to-all-done.3
  1570.7 7.6 all-to-all-start.4
  1579.8 7.6 all-to-all-done.4
  (176 shorter events, 131.4 us)
Async XLA Ops:
  7.2 24.5 %copy-start = (f32[32,8]{0,1:T(8,128)S(1)}, f32[32,8]{0,1:T(8,128)}, u32[]{:S(2)}) copy-start(f32[32,8]{0,1:T(8,128)} %param.29) | copy-start | bytes 3076
  7.2 10.2 copy-start.3
  7.2 330.1 %all-gather.5.cloned.1.call-start = ((), (), s32[]{:S(2)}) async-start(), calls=%async_computation.6 | async-start | bytes 6389760 | tf_op jit(solution)/shard_map/all_gather | solution.py:36
  8.8 678.0 %all-gather.7.cloned.1.call-start = ((), (), s32[]{:S(2)}) async-start(), calls=%async_computation.7 | async-start | bytes 2129920 | tf_op jit(solution)/shard_map/all_gather | solution.py:167
  9.5 1080.8 %all-gather.9.cloned.1.call-start = ((), (), s32[]{:S(2)}) async-start(), calls=%async_computation.8 | async-start | bytes 10649600 | tf_op jit(solution)/shard_map/all_gather | solution.py:36
  21.1 59.3 %all-to-all-start = ((bf16[4,128,2048]{2,1,0:T(8,128)(2,1)}), bf16[4,128,2048]{2,1,0:T(8,128)(2,1)S(1)}, u32[]{:S(2)}, u32[]{:S(2)}) async-start(bf16[4,128,2048]{2,1,0:T(8,128)(2,1)} %broadcast_in_dim.58), calls=%async_computation | async-start | bytes 4194304 | tf_op jit(solution)/shard_map/all_to_all | solution.py:21
  31.1 1409.2 %all-gather.11.cloned.1.call-start = ((), (), s32[]{:S(2)}) async-start(), calls=%async_computation.9 | async-start | bytes 5324800 | tf_op jit(solution)/shard_map/all_gather | solution.py:182
  358.6 1.6 slice-start
  363.1 1.2 slice-start.1
  371.6 1.6 slice-start
  376.1 1.2 slice-start.1
  384.6 1.6 slice-start
  397.5 1.6 slice-start
  402.0 1.2 slice-start.1
  410.5 1.6 slice-start
  423.5 1.6 slice-start
  436.5 1.6 slice-start
  449.4 1.6 slice-start
  691.2 124.7 %all-to-all-start.1 = ((bf16[4,128,2048]{2,1,0:T(8,128)(2,1)}), bf16[4,128,2048]{2,1,0:T(8,128)(2,1)}, u32[]{:S(2)}, u32[]{:S(2)}) async-start(bf16[4,128,2048]{2,1,0:T(8,128)(2,1)} %bitcast.15), calls=%async_computation.1 | async-start | bytes 4194304 | tf_op jit(solution)/shard_map/all_to_all | solution.py:47
  777.9 775.3 %reduce-scatter.2.cloned.1.call-start = ((), (), s32[]{:S(2)}) async-start(), calls=%async_computation.10 | async-start | bytes 2621440 | tf_op jit(solution)/shard_map/reduce_scatter | solution.py:185
  818.4 1.2 copy-start.2
  1557.7 11.0 all-to-all-start.3
  1561.8 28.7 %copy-start.1 = (f32[32,8]{0,1:T(8,128)S(1)}, f32[32,8]{0,1:T(8,128)}, u32[]{:S(2)}) copy-start(f32[32,8]{0,1:T(8,128)} %param.29) | copy-start | bytes 3076
  1570.7 16.7 %all-to-all-start.4 = ((f32[64,1,2]{2,1,0:T(1,128)}), f32[64,1,2]{2,1,0:T(1,128)S(1)}, u32[]{:S(2)}, u32[]{:S(2)}) async-start(f32[64,1,2]{2,1,0:T(1,128)} %broadcast_in_dim.88), calls=%async_computation.5 | async-start | bytes 65536 | tf_op jit(solution)/shard_map/all_to_all | solution.py:21
  (6 other events, 6.8 us)
Sparse Core Ops, SparseCore 0:
  10.4 326.9 all-gather.4
  339.1 347.6 all-gather.6
  688.6 401.7 all-gather.8
  1092.0 348.2 all-gather.10
  1453.6 99.5 reduce-scatter.1
where the time goes:
time: 1600 us
  waiting for transfers between devices  1250 us (78%)
  starting transfers between devices  108 us (7%)
  local copies, waits for them, and re-layouts  95.1 us (6%)
  matrix products  63.7 us (4%)
  blocking collectives  44.2 us (3%)
  between operations  18.8 us (1%)
  other arithmetic  16.4 us (1%)
    all_gather x2, waiting for transfers between devices, in_one_piece(): lax.all_gather(both, axis, axis=dim, tiled=True)  483 us
    all_gather x1, waiting for transfers between devices, local(): lax.all_gather(w_down, 'dp', axis=1, tiled=True)  342 us
    all_gather x1, waiting for transfers between devices, local(): lax.all_gather(w_out, 'dp', axis=1, tiled=True)  227 us
    reduce_scatter x1, waiting for transfers between devices, local(): lax.psum_scatter(feed_partial, 'tensor', scatter_dimension=0, tiled=True)  98.7 us
    all_to_all x1, starting transfers between devices, sent_and_summed(): parts = lax.all_to_all(cut_along(array, dim, peers), axis, 0, 0, tiled=True)  86.6 us
    all_to_all x3, waiting for transfers between devices, from_everyone(): lax.all_to_all(jnp.broadcast_to(array[None], (peers, *array.shape)), axis...  62.2 us
    all_to_all x1, blocking collectives, from_everyone(): lax.all_to_all(jnp.broadcast_to(array[None], (peers, *array.shape)), axis...  44.2 us
    all_to_all x1, waiting for transfers between devices, sent_and_summed(): parts = lax.all_to_all(cut_along(array, dim, peers), axis, 0, 0, tiled=True)  36.7 us
  transfers between devices with their start and end apart: 9, of which 9 were waited for; matrix products, arithmetic and copies ran while one was open for 8% of the time, Pallas kernels for 0%

commit v1 on v0

--- a/solution.py
+++ b/solution.py
@@ -2,9 +2,107 @@
 import jax.numpy as jnp
 from jax import lax
 from jax.sharding import PartitionSpec as P
+from jax.experimental import pallas as pl
+from jax.experimental.pallas import tpu as pltpu
 
 DK = 64
 LEN = 512
+
+
+MESH = pl.DeviceIdType.MESH
+CH = (768, 256, 640, 640, 640)
+NC = len(CH)
+
+def coords():
+    d = lax.axis_index("dp"); t = lax.axis_index("tensor")
+    return d // 16, (d // 4) % 4, d % 4, t // 2, t % 2
+
+def did(z, x, y, h, c):
+    return {"dp": z * 16 + x * 4 + y, "tensor": h * 2 + c}
+
+def gather_kernel(*refs):
+    src = refs[: 2 * NC]; gb = refs[2 * NC: 4 * NC]
+    send_sem, recv_sem, loc_sem = refs[4 * NC:]
+    z, x, y, h, c = coords()
+    barrier = pltpu.get_barrier_semaphore()
+    peers = [did((z + k) % 4, x, y, h, c) for k in (1, 2, 3)]
+    peers += [did(z, (x + k) % 4, y, h, c) for k in (1, 3)]
+    peers += [did(z, x, (y + k) % 4, h, c) for k in (1, 3)]
+    for p in peers:
+        pl.semaphore_signal(barrier, inc=1, device_id=p, device_id_type=MESH)
+    pl.semaphore_wait(barrier, len(peers))
+    base = (y * 16 + x * 4, x * 16 + y * 4)
+    my1 = (x, y); my2 = (y, x)
+
+    def nb(col, ph, k):
+        if (col == 0) == (ph == 1):
+            return did(z, (x + k) % 4, y, h, c)
+        return did(z, x, (y + k) % 4, h, c)
+
+    def sec(col, ph, k):
+        if ph == 1:
+            return my2[col] * 16 + ((my1[col] + k) % 4) * 4
+        return ((my2[col] + k) % 4) * 16
+
+    def send(col, ch, start, size, slot, dev):
+        g = gb[col * NC + ch]
+        pltpu.make_async_remote_copy(src_ref=g.at[pl.ds(start, size)], dst_ref=g.at[pl.ds(start, size)],
+            send_sem=send_sem.at[col, ch], recv_sem=recv_sem.at[col, ch, slot],
+            device_id=dev, device_id_type=MESH).start()
+
+    def wait_recv(col, ch, slot, size):
+        g = gb[col * NC + ch]
+        pltpu.make_async_copy(g.at[pl.ds(0, size)], g.at[pl.ds(0, size)], recv_sem.at[col, ch, slot]).wait()
+
+    def level(col, ch, lv):
+        g = gb[col * NC + ch]; s = src[col * NC + ch]
+        if lv == 0:
+            mine = base[col] + z
+            pltpu.make_async_copy(s, g.at[mine], loc_sem.at[col, ch]).start()
+            for k in (1, 2, 3):
+                pltpu.make_async_remote_copy(src_ref=s, dst_ref=g.at[mine], send_sem=send_sem.at[col, ch],
+                    recv_sem=recv_sem.at[col, ch, 0], device_id=did((z + k) % 4, x, y, h, c), device_id_type=MESH).start()
+        elif lv in (1, 3):
+            ph = 1 if lv == 1 else 2
+            if ph == 1:
+                pltpu.make_async_copy(s, g.at[0], loc_sem.at[col, ch]).wait()
+                wait_recv(col, ch, 0, 3)
+            else:
+                wait_recv(col, ch, 3, 4)
+            size = 4 if ph == 1 else 16
+            b = 1 if ph == 1 else 4
+            for j, k in ((0, 1), (1, 3)):
+                send(col, ch, sec(col, ph, 0), size, b + j, nb(col, ph, k))
+        elif lv in (2, 4):
+            ph = 1 if lv == 2 else 2
+            size = 4 if ph == 1 else 16
+            b = 1 if ph == 1 else 4
+            half = size // 2
+            wait_recv(col, ch, b, size)
+            send(col, ch, sec(col, ph, 3), half, b + 2, nb(col, ph, 1))
+            wait_recv(col, ch, b + 1, size)
+            send(col, ch, sec(col, ph, 1) + half, half, b + 2, nb(col, ph, 3))
+        else:
+            wait_recv(col, ch, 6, 16)
+
+    for t in range(NC + 5):
+        for ch in range(NC):
+            if 0 <= t - ch <= 5:
+                for col in (0, 1):
+                    level(col, ch, t - ch)
+    for ch in range(NC):
+        for col in (0, 1):
+            g = gb[col * NC + ch]
+            pltpu.make_async_copy(g.at[pl.ds(0, 63)], g.at[pl.ds(0, 63)], send_sem.at[col, ch]).wait()
+
+
+ANY = pl.BlockSpec(memory_space=pl.ANY)
+VM = pl.BlockSpec(memory_space=pltpu.VMEM)
+def gather(*srcs):
+    outs = [jax.ShapeDtypeStruct((64, 32, n), jnp.bfloat16) for _ in range(2) for n in CH]
+    return pl.pallas_call(gather_kernel, out_shape=outs, in_specs=[ANY] * (2 * NC), out_specs=[VM] * (2 * NC),
+        scratch_shapes=[pltpu.SemaphoreType.DMA((2, NC)), pltpu.SemaphoreType.DMA((2, NC, 7)), pltpu.SemaphoreType.DMA((2, NC))],
+        compiler_params=pltpu.CompilerParams(collective_id=0, has_side_effects=True, vmem_limit_bytes=60 << 20), name="gather")(*srcs)
 
 
 bucket_edges = (12, 16, 23, 32, 46, 64, 91)
@@ -107,11 +205,30 @@
     inverse = jnp.sum(
         block_ids[:, None] * (shard_order[:, None] == block_ids[None, :]).astype(jnp.int32), axis=0
     )
-    own_rows = reorder_blocks(hidden_states, shard_order)
-    attn_gain = reorder_blocks(gain_attn, shard_order)
-    feed_gain = reorder_blocks(gain_ff, shard_order)
-    final_gain = reorder_blocks(gain_final, shard_order)
-    reward_head = reorder_blocks(w_reward, shard_order)
+    own_rows, attn_gain, feed_gain, final_gain, reward_head = (
+        hidden_states, gain_attn, gain_ff, gain_final, w_reward)
+    out_t, down_t = w_out.T, w_down.T
+    halves = []
+    for col in (0, 1):
+        h = slice(col * 256, col * 256 + 256)
+        half = slice(col * 640, col * 640 + 640)
+        big = (w_gate, w_up)[col]
+        halves += [jnp.concatenate([w_query[:, h], w_key[:, h], w_value[:, h]], axis=1), out_t[:, h],
+                   big[:, :640], big[:, 640:], down_t[:, half]]
+    got = gather(*halves)
+    zs, xs, ys = inverse // 16, (inverse // 4) % 4, inverse % 4
+    where = (ys * 16 + xs * 4 + zs, xs * 16 + ys * 4 + zs)
+
+    def true(col, ch):
+        blocks = jnp.take(got[col * NC + ch], where[col], axis=0)
+        return blocks.reshape(64 * 32, blocks.shape[2])
+
+    qkv = [true(0, 0), true(1, 0)]
+    full = [jnp.concatenate([q[:, i * 256:(i + 1) * 256] for q in qkv], axis=1) for i in range(3)]
+    out_full = jnp.concatenate([true(0, 1), true(1, 1)], axis=1)
+    gate_full = jnp.concatenate([true(0, 2), true(0, 3)], axis=1)
+    up_full = jnp.concatenate([true(1, 2), true(1, 3)], axis=1)
+    down_full = jnp.concatenate([true(0, 4), true(1, 4)], axis=1)
     row_count = own_rows.shape[0]
     row_start = lax.axis_index("tensor") * row_count
     normed = gather_directly(rms_norm(own_rows, attn_gain).astype(jnp.bfloat16), "tensor", 0)
@@ -127,7 +244,7 @@
     zero_block = jnp.zeros((LEN, inner_width), jnp.float32)
     attn_contract = contract_with(normed)
     running = (zero_block, zero_block, zero_block)
-    portion = in_one_piece((w_query, w_key, w_value), "dp", 0, 1)
+    portion = full
     offset = jnp.int32(0)
     queries = attn_contract(running[0], portion[0], offset)
     key_states = attn_contract(running[1], portion[1], offset)
@@ -164,7 +281,7 @@
     context = lax.map(head_step, (query_heads, key_heads, value_heads, offset_bias))
     context = context.transpose(1, 0, 2).reshape(LEN, inner_width)
     attn_partial = jnp.dot(
-        context, lax.all_gather(w_out, "dp", axis=1, tiled=True), preferred_element_type=jnp.float32
+        context, out_full.T, preferred_element_type=jnp.float32
     ).astype(jnp.bfloat16)
     mid_own = own_rows + sent_and_summed(attn_partial, "tensor", 0)
     mid_normed = gather_directly(rms_norm(mid_own, feed_gain).astype(jnp.bfloat16), "tensor", 0)
@@ -172,14 +289,14 @@
     zero_hidden = jnp.zeros((LEN, hidden_width), jnp.float32)
     feed_contract = contract_with(mid_normed)
     running = (zero_hidden, zero_hidden)
-    portion = in_one_piece((w_gate, w_up), "dp", 0, 1)
+    portion = (gate_full, up_full)
     offset = jnp.int32(0)
     gate_proj = feed_contract(running[0], portion[0], offset)
     up_proj = feed_contract(running[1], portion[1], offset)
     activated = (jax.nn.gelu(gate_proj, approximate=True) * up_proj).astype(jnp.bfloat16)
     feed_partial = jnp.dot(
         activated,
-        lax.all_gather(w_down, "dp", axis=1, tiled=True),
+        down_full.T,
         preferred_element_type=jnp.float32,
     ).astype(jnp.bfloat16)
     output_rows = mid_own + lax.psum_scatter(
@@ -196,7 +313,7 @@
     reward_mean = first_moment / rollouts
     reward_var = second_moment / rollouts - reward_mean * reward_mean
     normalized = (reward - reward_mean) / jnp.sqrt(reward_var + 1e-06)
-    return (reorder_blocks(output_rows, inverse), normalized)
+    return (output_rows, normalized)
 
 
 def solution(mesh):

time: 1600 us -> 597 us (0.37)
  waiting for transfers between devices: 1250 us -> 73.5 us
  Pallas kernels: 0 us -> 188 us
  starting transfers between devices: 108 us -> 25 us
  blocking collectives: 44.2 us -> 75.6 us
  local copies, waits for them, and re-layouts: 95.1 us -> 124 us
    all_gather x4 -> x0, waiting for transfers between devices: 1050 us -> none  [the longest x2 483 us: in_one_piece(): lax.all_gather(both, axis, axis=dim, tiled=True)]
    pallas_call x0 -> x1, Pallas kernels: none -> 188 us  [gather(): pl.pallas_call(gather_kernel, out_shape=outs, in_specs=[ANY] * (2 * NC),...]
    all_to_all x1 -> x0, starting transfers between devices: 86.6 us -> none  [sent_and_summed(): parts = lax.all_to_all(cut_along(array, dim, peers), axis, 0, 0, tiled=True)]
    all_to_all x3 -> x2, waiting for transfers between devices: 62.2 us -> 0.74 us  [from_everyone(): lax.all_to_all(jnp.broadcast_to(array[None], (peers, *array.shape)), axis...]
    all_to_all x0 -> x1, blocking collectives: none -> 48.3 us  [sent_and_summed(): parts = lax.all_to_all(cut_along(array, dim, peers), axis, 0, 0, tiled=True)]
    all_to_all x1 -> x0, waiting for transfers between devices: 36.7 us -> none  [sent_and_summed(): parts = lax.all_to_all(cut_along(array, dim, peers), axis, 0, 0, tiled=True)]
    gather x6 -> x10, local copies, waits for them, and re-layouts: 3.65 us -> 32.5 us  [true(): blocks = jnp.take(got[col * NC + ch], where[col], axis=0)]
    reduce_scatter x1, waiting for transfers between devices: 98.7 us -> 72.8 us  [local(): lax.psum_scatter(feed_partial, 'tensor', scatter_dimension=0, tiled=True)]
  transfers between devices with their start and end apart: 9 -> 3, of which waited for: 9 -> 2; matrix products, arithmetic and copies ran while one was open for 8% -> 9% of each run, Pallas kernels for 0% -> 32%
where the time goes in v1:
time: 597 us; the launch traced here: 595 us
  Pallas kernels  188 us (31%)
  local copies, waits for them, and re-layouts  124 us (21%)
  blocking collectives  75.6 us (13%)
  waiting for transfers between devices  73.5 us (12%)
  matrix products  62 us (10%)
  other arithmetic  27.5 us (5%)
  starting transfers between devices  25 us (4%)
  between operations  19.3 us (3%)
    pallas_call x1, Pallas kernels, gather(): pl.pallas_call(gather_kernel, out_shape=outs, in_specs=[ANY] * (2 * NC),...  188 us
    reduce_scatter x1, waiting for transfers between devices, local(): lax.psum_scatter(feed_partial, 'tensor', scatter_dimension=0, tiled=True)  72.8 us
    all_to_all x1, blocking collectives, sent_and_summed(): parts = lax.all_to_all(cut_along(array, dim, peers), axis, 0, 0, tiled=True)  48.3 us
    gather x10, local copies, waits for them, and re-layouts, true(): blocks = jnp.take(got[col * NC + ch], where[col], axis=0)  32.5 us
    all_to_all x2, blocking collectives, from_everyone(): lax.all_to_all(jnp.broadcast_to(array[None], (peers, *array.shape)), axis...  27.3 us
    all_to_all x2, starting transfers between devices, from_everyone(): lax.all_to_all(jnp.broadcast_to(array[None], (peers, *array.shape)), axis...  25 us
    another operation x16, local copies, waits for them, and re-layouts, head_step(): jnp.tile(head_offsets, LEN)[:LEN * (span - 1)].reshape(LEN, span - 1)  23.3 us
    reshape x8, local copies, waits for them, and re-layouts, head_step(): jnp.tile(head_offsets, LEN)[:LEN * (span - 1)].reshape(LEN, span - 1)  23.2 us
  transfers between devices with their start and end apart: 3, of which 2 were waited for; matrix products, arithmetic and copies ran while one was open for 9% of the time, Pallas kernels for 32%

profile of v1, /device:TPU:1, one launch (start us, length us, event | category | flops | bytes accessed | tf_op | source)
XLA Modules:
  0.0 595.4 jit_solution(16111911723310262880)
XLA Ops:
  11.7 10.1 %all-to-all-start = ((bf16[4,128,2048]{2,1,0:T(8,128)(2,1)}), bf16[4,128,2048]{2,1,0:T(8,128)(2,1)}, u32[]{:S(2)}, u32[]{:S(2)}) async-start(bf16[4,128,2048]{2,1,0:T(8,128)(2,1)} %broadcast_in_dim.67), calls=%async_computation | async-start | bytes 4194304 | tf_op jit(solution)/shard_map/all_to_all | solution.py:119
  24.6 188.2 %gather.47 = (bf16[64,32,768]{2,1,0:T(8,128)(2,1)}, bf16[64,32,256]{2,1,0:T(8,128)(2,1)}, bf16[64,32,640]{2,1,0:T(8,128)(2,1)}, bf16[64,32,640]{2,1,0:T(8,128)(2...) custom-call(bf16[32,768]{1,0:T(8,128)(2,1)} %get-tuple-element.135.r, ...), custom_call_target="tpu_custom_call" | custom-call | tf_op jit(solution)/shard_map/gather/pallas_call | solution.py:103
  218.2 4.3 gather_fusion
  234.4 4.3 fusion.59
  241.1 3.9 fusion.62
  246.6 3.8 fusion.65
  252.7 103.3 %while.11 = (s32[]{:T(128)}, bf16[8,512,64]{1,2,0:T(8,128)(2,1)}, bf16[8,512,64]{2,1,0:T(8,128)(2,1)}, bf16[8,512,64]{2,1,0:T(8,128)(2,1)S(1)}, f32[8,1023]{1,0:...) while((s32[]{:T(128)}, bf16[8,512,64]{1,2,0:T(8,128)(2,1)}, ...), condition=%wide.region_5.7_spmd.clone, body=%wide.region_2.6_spmd.clone.sunk | while | flops 69238272 | bytes 26672256 | solution.py:281
  270.2 2.9 reshape.305
  283.1 2.9 reshape.305
  296.0 2.9 reshape.305
  308.9 2.9 reshape.305
  356.0 3.0 convolution_convert_fusion.1
  359.1 48.3 %all_to_all.27 = bf16[4,128,2048]{2,1,0:T(8,128)(2,1)S(1)} all-to-all(bf16[4,128,2048]{2,1,0:T(8,128)(2,1)S(1)} %bitcast.84), channel_id=1, replica_groups=mesh['dp'=64,'tensor'=4] {'tensor'}, dimensions={0} | all-to-all | bytes 4194304 | tf_op jit(solution)/shard_map/all_to_all | solution.py:145
  411.6 14.9 %all-to-all-start.2 = ((bf16[4,128,2048]{2,1,0:T(8,128)(2,1)}), bf16[4,128,2048]{2,1,0:T(8,128)(2,1)}, u32[]{:S(2)}, u32[]{:S(2)}) async-start(bf16[4,128,2048]{2,1,0:T(8,128)(2,1)} %broadcast_in_dim.97), calls=%async_computation.2 | async-start | bytes 4194304 | tf_op jit(solution)/shard_map/all_to_all | solution.py:119
  428.9 4.2 gather_fusion.5
  438.2 4.1 gather_fusion.7
  442.3 4.1 gather_fusion.9
  446.4 6.6 %broadcast_select_fusion.7 = (bf16[64,32,640]{2,1,0:T(8,128)(2,1)}, bf16[64,32,640]{2,1,0:T(8,128)(2,1)}, bf16[64,32,640]{2,1,0:T(8,128)(2,1)}) fusion(bf16[64,32,640]{2,1,0:T(8,128)(2,1)} %gather_fusion.4, pred[64]{0:T(512)(128)(4,1)S(1)} %get-tuple-element.98, bf16[64,32,640]{2,1,0:T(8,128)(2,1)} %gather_fusion.5, bf16[64,32,640]{2,1,0:T(8,128)(2,1)} %gather_fusion.8), kind=kLoop, calls=%fused_computation.61 | loop fusion | flops 3932160 | bytes 15728704 | tf_op jit(solution)/shard_map/jit(_take)/select_n | solution.py:223
  454.0 3.5 broadcast_select_fusion.4
  458.2 8.0 %fusion.41 = f32[512,1280]{1,0:T(8,128)} fusion(bf16[512,2048]{1,0:T(8,128)(2,1)} %bitcast.18, bf16[2048,640]{1,0:T(8,128)(2,1)} %bitcast.80, bf16[2048,640]{1,0:T(8,128)(2,1)} %bitcast.79), kind=kOutput, calls=%fused_computation.55 | convolution fusion | flops 2700083200 | bytes 9961472 | tf_op jit(solution)/shard_map/dot_general | solution.py:239
  466.2 12.4 %fusion.32 = bf16[512,2048]{1,0:T(8,128)(2,1)} fusion(bf16[2048,640]{1,0:T(8,128)(2,1)} %bitcast.83, bf16[2048,640]{1,0:T(8,128)(2,1)S(1)} %bitcast.78, f32[512,1280]{1,0:T(8,128)} %fusion.41, bf16[512,2048]{1,0:T(8,128)(2,1)} %bitcast.18, bf16[2048,640]{1,0:T(8,128)(2,1)} %bitcast.82, bf16[2048,640]{1,0:T(8,128)(2,1)} %bitcast.81), kind=kOutput, calls=%fused_computation.47 | convolution fusion | flops 5392039936 | bytes 17301504 | tf_op jit(solution)/shard_map/dot_general | solution.py:297
  479.3 72.8 %reduce-scatter.2.cloned.1.call-done = bf16[128,2048]{1,0:T(8,128)(2,1)} async-done(((bf16[512,2048]{1,0:T(8,128)(2,1)}), bf16[128,2048]{1,0:T(8,128)(2,1)}) %reduce-scatter.2.cloned.1.call-update) | async-done | bytes 524304 | tf_op jit(solution)/shard_map/reduce_scatter | solution.py:302
  555.6 10.2 %all_to_all.28 = f32[4,1,1]{2,1,0:T(1,128)S(1)} all-to-all(f32[4,1,1]{2,1,0:T(1,128)S(1)} %broadcast_in_dim.99), channel_id=1, replica_groups=mesh['dp'=64,'tensor'=4] {'tensor'}, dimensions={0} | all-to-all | bytes 32 | tf_op jit(solution)/shard_map/all_to_all | solution.py:119
  567.1 17.1 %all_to_all.29 = f32[64,1,2]{2,1,0:T(1,128)S(1)} all-to-all(f32[64,1,2]{2,1,0:T(1,128)S(1)} %broadcast_in_dim.100), channel_id=1, replica_groups=mesh['dp'=64,'tensor'=4] {'dp'}, dimensions={0} | all-to-all | bytes 1024 | tf_op jit(solution)/shard_map/all_to_all | solution.py:119
  (198 shorter events, 140.4 us)
Async XLA Ops:
  7.2 546.2 %copy-start = (f32[2048]{0:T(1024)S(1)}, f32[2048]{0:T(1024)}, u32[]{:S(2)}) copy-start(f32[2048]{0:T(1024)} %param.37) | copy-start | bytes 24580
  11.6 10.2 %copy-start.15 = (bf16[32,512]{1,0:T(8,128)(2,1)S(1)}, bf16[32,512]{1,0:T(8,128)(2,1)}, u32[]{:S(2)}) copy-start(bf16[32,512]{1,0:T(8,128)(2,1)} %param.27) | copy-start | bytes 98308
  11.6 10.2 %copy-start.16 = (bf16[32,512]{1,0:T(8,128)(2,1)S(1)}, bf16[32,512]{1,0:T(8,128)(2,1)}, u32[]{:S(2)}) copy-start(bf16[32,512]{1,0:T(8,128)(2,1)} %param.28) | copy-start | bytes 98308
  11.6 10.2 %copy-start.17 = (bf16[32,512]{1,0:T(8,128)(2,1)S(1)}, bf16[32,512]{1,0:T(8,128)(2,1)}, u32[]{:S(2)}) copy-start(bf16[32,512]{1,0:T(8,128)(2,1)} %param.29) | copy-start | bytes 98308
  11.6 10.2 %copy-start.14 = (bf16[32,1280]{1,0:T(8,128)(2,1)S(1)}, bf16[32,1280]{1,0:T(8,128)(2,1)}, u32[]{:S(2)}) copy-start(bf16[32,1280]{1,0:T(8,128)(2,1)} %param.33) | copy-start | bytes 245764
  11.6 10.9 %copy-start.18 = (bf16[512,32]{0,1:T(8,128)(2,1)S(1)}, bf16[512,32]{0,1:T(8,128)(2,1)}, u32[]{:S(2)}) copy-start(bf16[512,32]{0,1:T(8,128)(2,1)} %param.30) | copy-start | bytes 98308
  11.7 11.5 %copy-start.22 = (s32[64]{0:T(128)S(1)}, s32[64]{0:T(128)}, u32[]{:S(2)}) copy-start(s32[64]{0:T(128)} %param.25) | copy-start | bytes 772
  11.7 11.6 %copy-start.12 = (bf16[1280,32]{0,1:T(8,128)(2,1)S(1)}, bf16[1280,32]{0,1:T(8,128)(2,1)}, u32[]{:S(2)}) copy-start(bf16[1280,32]{0,1:T(8,128)(2,1)} %param.35) | copy-start | bytes 245764
  11.7 11.6 %copy-start.13 = (bf16[32,1280]{1,0:T(8,128)(2,1)S(1)}, bf16[32,1280]{1,0:T(8,128)(2,1)}, u32[]{:S(2)}) copy-start(bf16[32,1280]{1,0:T(8,128)(2,1)} %param.34) | copy-start | bytes 245764
  11.7 222.7 %all-to-all-start = ((bf16[4,128,2048]{2,1,0:T(8,128)(2,1)}), bf16[4,128,2048]{2,1,0:T(8,128)(2,1)}, u32[]{:S(2)}, u32[]{:S(2)}) async-start(bf16[4,128,2048]{2,1,0:T(8,128)(2,1)} %broadcast_in_dim.67), calls=%async_computation | async-start | bytes 4194304 | tf_op jit(solution)/shard_map/all_to_all | solution.py:119
  218.2 7.2 %copy-start.21 = (f32[32,8]{0,1:T(8,128)S(1)}, f32[32,8]{0,1:T(8,128)}, u32[]{:S(2)}) copy-start(f32[32,8]{0,1:T(8,128)} %param.31) | copy-start | bytes 3076
  225.4 2.9 copy-start.7
  229.4 1.9 copy-start.1
  407.4 2.4 copy-start.19
  411.6 14.9 %copy-start.10 = (bf16[64,32,640]{2,1,0:T(8,128)(2,1)S(1)}, bf16[64,32,640]{2,1,0:T(8,128)(2,1)}, u32[]{:S(2)}) copy-start(bf16[64,32,640]{2,1,0:T(8,128)(2,1)} %get-tuple-element.57) | copy-start | bytes 7864324
  411.6 46.6 %all-to-all-start.2 = ((bf16[4,128,2048]{2,1,0:T(8,128)(2,1)}), bf16[4,128,2048]{2,1,0:T(8,128)(2,1)}, u32[]{:S(2)}, u32[]{:S(2)}) async-start(bf16[4,128,2048]{2,1,0:T(8,128)(2,1)} %broadcast_in_dim.97), calls=%async_computation.2 | async-start | bytes 4194304 | tf_op jit(solution)/shard_map/all_to_all | solution.py:119
  426.5 125.6 %reduce-scatter.2.cloned.1.call-start = ((), (), s32[]{:S(2)}) async-start(), calls=%async_computation.6 | async-start | bytes 2621440 | tf_op jit(solution)/shard_map/reduce_scatter | solution.py:302
  428.9 4.2 copy-start.9
  446.4 6.6 %copy-start.2 = (bf16[64,32,640]{2,1,0:T(8,128)(2,1)S(1)}, bf16[64,32,640]{2,1,0:T(8,128)(2,1)}, u32[]{:S(2)}) copy-start(bf16[64,32,640]{2,1,0:T(8,128)(2,1)} %gather_fusion.7) | copy-start | bytes 7864324
  446.4 7.6 %copy-start.3 = (bf16[64,32,640]{2,1,0:T(8,128)(2,1)S(1)}, bf16[64,32,640]{2,1,0:T(8,128)(2,1)}, u32[]{:S(2)}) copy-start(bf16[64,32,640]{2,1,0:T(8,128)(2,1)} %gather_fusion.9) | copy-start | bytes 7864324
  458.2 8.0 %copy-start.11 = (bf16[64,32,640]{2,1,0:T(8,128)(2,1)S(1)}, bf16[64,32,640]{2,1,0:T(8,128)(2,1)}, u32[]{:S(2)}) copy-start(bf16[64,32,640]{2,1,0:T(8,128)(2,1)} %get-tuple-element.134) | copy-start | bytes 7864324
  478.6 73.5 %copy-start.6 = (f32[128,2048]{1,0:T(8,128)S(1)}, f32[128,2048]{1,0:T(8,128)}, u32[]{:S(2)}) copy-start(f32[128,2048]{1,0:T(8,128)} %copy-done.5) | copy-start | bytes 3145732
  478.6 74.8 %copy-start.20 = (f32[2048]{0:T(1024)S(1)}, f32[2048]{0:T(1024)}, u32[]{:S(2)}) copy-start(f32[2048]{0:T(1024)} %param.36) | copy-start | bytes 24580
  553.4 34.0 %copy-start.8 = (f32[128,2048]{1,0:T(8,128)}, f32[128,2048]{1,0:T(8,128)S(1)}, u32[]{:S(2)}) copy-start(f32[128,2048]{1,0:T(8,128)S(1)} %get-tuple-element.95) | copy-start | bytes 3145732
  (18 other events, 24.7 us)
Sparse Core Ops, SparseCore 0:
  478.7 73.3 reduce-scatter.1

commit v2 on v0

v2 whole, which is shorter than its diff:
```python
import jax
import jax.numpy as jnp
from jax import lax
from jax.sharding import PartitionSpec as P
from jax.experimental import pallas as pl
from jax.experimental.pallas import tpu as pltpu

DK = 64
LEN = 512
D = 2048
ROWS = 128
MESH = pl.DeviceIdType.MESH
BF = jnp.bfloat16
F32 = jnp.float32
CH = (768, 256, 768, 512, 640)
NC = len(CH)
GA, GF = 2, 4
bucket_edges = (12, 16, 23, 32, 46, 64, 91)


def coords():
    d = lax.axis_index("dp")
    t = lax.axis_index("tensor")
    return d // 16, (d // 4) % 4, d % 4, t // 2, t % 2


def did(z, x, y, h, c):
    return {"dp": z * 16 + x * 4 + y, "tensor": h * 2 + c}


def rms(v, gain):
    return v * lax.rsqrt(jnp.mean(v * v, axis=-1, keepdims=True) + 1e-06) * gain


def nt(a, b):
    return lax.dot_general(a, b, (((1,), (1,)), ((), ())), preferred_element_type=F32)


def layer_kernel(*refs):
    (pos, length_ref, rel, hidden, gains), refs = refs[:5], refs[5:]
    src, refs = refs[: 2 * NC], refs[2 * NC :]
    (out, norm_out), refs = refs[:2], refs[2:]
    gb, refs = refs[: 2 * NC], refs[2 * NC :]
    (nbuf, mbuf, bias, qkv, ctx, act, part, mid, s1a, r1a, s2a, r2a, s1f, r1f, s2f, r2f, ra, rb) = refs[:18]
    send_sem, recv_sem, loc_sem, ag_send, ag_recv, ea_send, ea_recv, ef_send, ef_recv, rw_send, rw_recv = refs[18:]
    z, x, y, h, c = coords()
    me = h * 2 + c
    sib, far = did(z, x, y, h, 1 - c), did(z, x, y, 1 - h, c)
    i_sib, i_far, i_farsib = h * 2 + 1 - c, (1 - h) * 2 + c, (1 - h) * 2 + 1 - c
    length = length_ref[0]

    line = h * 8 + z * 2 + c
    plane = x * 4 + y

    def line_peer(k):
        i = (line + k) % 16
        return did((i // 2) % 4, x, y, i // 8, i % 2)

    def plane_peer(k):
        i = (plane + k) % 16
        return did(z, i // 4, i % 4, h, c)

    barrier = pltpu.get_barrier_semaphore()
    for k in range(1, 16):
        pl.semaphore_signal(barrier, inc=1, device_id=line_peer(k), device_id_type=MESH)
        pl.semaphore_signal(barrier, inc=1, device_id=plane_peer(k), device_id_type=MESH)
    pl.semaphore_wait(barrier, 30)

    base = (y * 16 + x * 4, x * 16 + y * 4)
    ring1, ring2 = (x, y), (y, x)

    def remote(s, d, ss, rs, dev):
        return pltpu.make_async_remote_copy(
            src_ref=s, dst_ref=d, send_sem=ss, recv_sem=rs, device_id=dev, device_id_type=MESH
        )

    def ring_peer(col, ph, k):
        if (col == 0) == (ph == 1):
            return did(z, (x + k) % 4, y, h, c)
        return did(z, x, (y + k) % 4, h, c)

    def section(col, ph, k):
        if ph == 1:
            return ring2[col] * 16 + ((ring1[col] + k) % 4) * 4
        return ((ring2[col] + k) % 4) * 16

    def send(col, ch, start, size, slot, dev):
        g = gb[col * NC + ch]
        s = g.at[pl.ds(start, size)]
        remote(s, s, send_sem.at[col, ch], recv_sem.at[col, ch, slot], dev).start()

    def arrived(ref, sem):
        pltpu.make_async_copy(ref, ref, sem).wait()

    def came(col, ch, slot, size):
        arrived(gb[col * NC + ch].at[pl.ds(0, size)], recv_sem.at[col, ch, slot])

    def level(col, ch, lv):
        g, s = gb[col * NC + ch], src[col * NC + ch]
        if lv == 0:
            mine = base[col] + z
            pltpu.make_async_copy(s, g.at[mine], loc_sem.at[col, ch]).start()
            for k in (1, 2, 3):
                remote(
                    s, g.at[mine], send_sem.at[col, ch], recv_sem.at[col, ch, 0], did((z + k) % 4, x, y, h, c)
                ).start()
        elif lv in (1, 3):
            ph = 1 if lv == 1 else 2
            if ph == 1:
                pltpu.make_async_copy(s, g.at[0], loc_sem.at[col, ch]).wait()
                came(col, ch, 0, 3)
            else:
                came(col, ch, 3, 4)
            size, b = (4, 1) if ph == 1 else (16, 4)
            for j, k in ((0, 1), (1, 3)):
                send(col, ch, section(col, ph, 0), size, b + j, ring_peer(col, ph, k))
        elif lv in (2, 4):
            ph = 1 if lv == 2 else 2
            size, b = (4, 1) if ph == 1 else (16, 4)
            half = size // 2
            came(col, ch, b, size)
            send(col, ch, section(col, ph, 3), half, b + 2, ring_peer(col, ph, 1))
            came(col, ch, b + 1, size)
            send(col, ch, section(col, ph, 1) + half, half, b + 2, ring_peer(col, ph, 3))
        else:
            came(col, ch, 6, 16)

    def wave(t):
        for ch in range(NC):
            if 0 <= t - ch <= 5:
                for col in (0, 1):
                    level(col, ch, t - ch)

    def spread(buf, n):
        to_sib = remote(buf.at[me], buf.at[me], ag_send.at[n, 0], ag_recv.at[n, 0], sib)
        to_far = remote(buf.at[me], buf.at[me], ag_send.at[n, 1], ag_recv.at[n, 1], far)
        to_far.start()
        to_sib.start()

    def pass_on(buf, n):
        arrived(buf.at[0], ag_recv.at[n, 1])
        remote(buf.at[i_far], buf.at[i_far], ag_send.at[n, 2], ag_recv.at[n, 2], sib).start()

    def spread_end(buf, n):
        arrived(buf.at[0], ag_recv.at[n, 0])
        arrived(buf.at[0], ag_recv.at[n, 2])

    def to_sibling(g, width, s1, r1, ss, rs):
        cols = slice(g * width, (g + 1) * width)
        s1[g, 0] = part[i_sib, :, cols].astype(BF)
        s1[g, 1] = part[i_farsib, :, cols].astype(BF)
        remote(s1.at[g], r1.at[g], ss.at[0, g], rs.at[0, g], sib).start()

    def to_far(g, width, r1, s2, r2, ss, rs):
        cols = slice(g * width, (g + 1) * width)
        arrived(r1.at[g], rs.at[0, g])
        s2[g] = (part[i_far, :, cols] + r1[g, 1].astype(F32)).astype(BF)
        remote(s2.at[g], r2.at[g], ss.at[1, g], rs.at[1, g], far).start()

    def total(g, width, r1, r2, rs):
        cols = slice(g * width, (g + 1) * width)
        arrived(r2.at[g], rs.at[1, g])
        return part[me, :, cols] + r1[g, 0].astype(F32) + r2[g].astype(F32)

    def blocks(col, ch, first, count, cols):
        g = gb[col * NC + ch]
        return jnp.concatenate([g[pos[col, first + b], :, cols] for b in range(count)], axis=0)

    wave(0)
    nbuf[me] = rms(hidden[...], gains[0:1]).astype(BF)
    spread(nbuf, 0)
    wave(1)

    row = lax.broadcasted_iota(jnp.int32, (ROWS, ROWS), 0)
    lane = lax.broadcasted_iota(jnp.int32, (ROWS, ROWS), 1)

    def bias_tile(n, _):
        for o in range(3):
            r = (o - 1) * ROWS + lane - row
            dist = jnp.abs(r)
            low = jnp.minimum(dist, 8)
            for edge in bucket_edges:
                low = low + (dist >= edge).astype(jnp.int32)
            bucket = jnp.where(r > 0, 16, 0) + low
            tile = jnp.zeros((ROWS, ROWS), F32)
            for b in range(32):
                tile = jnp.where(bucket == b, rel[b, n], tile)
            bias[n, o] = tile
        return 0

    lax.fori_loop(0, 8, bias_tile, 0)
    wave(2)
    wave(3)
    pass_on(nbuf, 0)
    wave(4)
    spread_end(nbuf, 0)
    wave(5)

    for col in (0, 1):
        def qkv_tile(i, _):
            cols = pl.ds(pl.multiple_of(i * 256, 256), 256)
            w = blocks(col, 0, 0, 64, cols)
            qkv[col, :, cols] = jnp.dot(
                nbuf[...].reshape(LEN, D), w, preferred_element_type=F32
            ).astype(BF)
            return 0

        lax.fori_loop(0, 3, qkv_tile, 0)

    lane_q = lax.broadcasted_iota(jnp.int32, (ROWS, 128), 1)
    key_pos = lax.broadcasted_iota(jnp.int32, (ROWS, LEN), 1)
    valid = key_pos < length

    def heads(p, _):
        col = p // 2
        at = (p % 2) * 128
        q_cols = pl.ds(pl.multiple_of(at, 128), 128)
        k_cols = pl.ds(pl.multiple_of(at + 256, 128), 128)
        v_cols = pl.ds(pl.multiple_of(at + 512, 128), 128)
        keys = qkv[col, :, k_cols]
        values = qkv[col, :, v_cols]
        for qt in range(4):
            q = qkv[col, qt * ROWS : (qt + 1) * ROWS, q_cols]
            got = []
            for hh in (0, 1):
                n = p * 2 + hh
                q_head = jnp.where((lane_q >= 64) == (hh == 1), q, jnp.zeros_like(q))
                s = nt(q_head, keys)
                tiles = []
                for kt in range(4):
                    if abs(kt - qt) <= 1:
                        tiles.append(bias[n, kt - qt + 1])
                    else:
                        tiles.append(jnp.full((ROWS, ROWS), rel[31 if kt > qt else 15, n], F32))
                s = jnp.where(valid, s + jnp.concatenate(tiles, axis=1), -1e30)
                e = jnp.exp(s - jnp.max(s, axis=-1, keepdims=True))
                pr = (e * (1.0 / jnp.sum(e, axis=-1, keepdims=True))).astype(BF)
                got.append(jnp.dot(pr, values, preferred_element_type=F32))
            c_cols = pl.ds(pl.multiple_of(p * 128, 128), 128)
            ctx[qt * ROWS : (qt + 1) * ROWS, c_cols] = jnp.where(lane_q < 64, got[0], got[1]).astype(BF)
        return 0

    lax.fori_loop(0, 2, heads, 0)
    wave(6)
    lax.fori_loop(2, 4, heads, 0)

    def out_tile(i, _):
        cols = pl.ds(pl.multiple_of(i * 256, 256), 256)
        all_ = slice(0, 256)
        s = nt(ctx[:, :256], blocks(0, 1, i * 8, 8, all_)) + nt(ctx[:, 256:], blocks(1, 1, i * 8, 8, all_))
        part[:, :, cols] = s.reshape(4, ROWS, 256)
        return 0

    wa = D // GA
    for g in range(GA):
        lax.fori_loop(g * (8 // GA), (g + 1) * (8 // GA), out_tile, 0)
        to_sibling(g, wa, s1a, r1a, ea_send, ea_recv)
    for g in range(GA):
        to_far(g, wa, r1a, s2a, r2a, ea_send, ea_recv)
    wave(7)
    for g in range(GA):
        cols = slice(g * wa, (g + 1) * wa)
        mid[:, cols] = hidden[:, cols] + total(g, wa, r1a, r2a, ea_recv)
    mbuf[me] = rms(mid[...], gains[1:2]).astype(BF)
    spread(mbuf, 1)
    wave(8)
    pass_on(mbuf, 1)
    spread_end(mbuf, 1)

    def feed_tile(ch, i, at):
        cols = pl.ds(pl.multiple_of(i * 256, 256), 256)
        lhs = mbuf[...].reshape(LEN, D)
        gate = jnp.dot(lhs, blocks(0, ch, 0, 64, cols), preferred_element_type=F32)
        up = jnp.dot(lhs, blocks(1, ch, 0, 64, cols), preferred_element_type=F32)
        act[:, pl.ds(pl.multiple_of(at + i * 256, 256), 256)] = (
            jax.nn.gelu(gate, approximate=True) * up
        ).astype(BF)
        return 0

    lax.fori_loop(0, 3, lambda i, _: feed_tile(2, i, 0), 0)
    lax.fori_loop(0, 2, lambda i, _: feed_tile(3, i, 768), 0)
    wave(9)

    def down_tile(i, _):
        cols = pl.ds(pl.multiple_of(i * 256, 256), 256)
        all_ = slice(0, 640)
        s = nt(act[:, :640], blocks(0, 4, i * 8, 8, all_)) + nt(act[:, 640:], blocks(1, 4, i * 8, 8, all_))
        part[:, :, cols] = s.reshape(4, ROWS, 256)
        return 0

    wf = D // GF
    for g in range(GF):
        lax.fori_loop(g * (8 // GF), (g + 1) * (8 // GF), down_tile, 0)
        to_sibling(g, wf, s1f, r1f, ef_send, ef_recv)
        if g > 0:
            to_far(g - 1, wf, r1f, s2f, r2f, ef_send, ef_recv)
    to_far(GF - 1, wf, r1f, s2f, r2f, ef_send, ef_recv)
    square = jnp.zeros((ROWS, 1), F32)
    dot = jnp.zeros((ROWS, 1), F32)
    for g in range(GF):
        cols = slice(g * wf, (g + 1) * wf)
        o = mid[:, cols] + total(g, wf, r1f, r2f, ef_recv)
        out[:, cols] = o
        square = square + jnp.sum(o * o, axis=-1, keepdims=True)
        dot = dot + jnp.sum(o * (gains[2:3, cols] * gains[3:4, cols]), axis=-1, keepdims=True)
    score = dot * lax.rsqrt(square * (1.0 / D) + 1e-06)
    at_row = lax.broadcasted_iota(jnp.int32, (ROWS, 1), 0) + me * ROWS
    pooled = jnp.sum(jnp.where(at_row < length, score, 0.0), axis=0, keepdims=True)

    ra[line] = jnp.broadcast_to(pooled / length.astype(F32), (8, 128))
    copies = []
    for k in range(1, 16):
        cp = remote(ra.at[line], ra.at[line], rw_send.at[0], rw_recv.at[0], line_peer(k))
        cp.start()
    arrived(ra.at[pl.ds(0, 15)], rw_recv.at[0])
    sub = lax.broadcasted_iota(jnp.int32, (8, 128), 0)
    tile = jnp.zeros((8, 128), F32)
    for k in range(4):
        tile = jnp.where(sub == k, ra[2 * k] + ra[2 * k + 1] + ra[8 + 2 * k] + ra[9 + 2 * k], tile)
    rb[plane] = tile
    for k in range(1, 16):
        remote(rb.at[plane], rb.at[plane], rw_send.at[1], rw_recv.at[1], plane_peer(k)).start()
    own = ra[2 * z] + ra[2 * z + 1] + ra[8 + 2 * z] + ra[9 + 2 * z]
    arrived(rb.at[pl.ds(0, 15)], rw_recv.at[1])
    every = jnp.sum(rb[...], axis=0)
    mean = jnp.sum(every, axis=0, keepdims=True) * (1.0 / 64)
    off = jnp.where((sub < 4)[None], rb[...] - mean[None], 0.0)
    var = jnp.sum(jnp.sum(off * off, axis=0), axis=0, keepdims=True) * (1.0 / 64)
    norm_out[...] = (own - mean) / jnp.sqrt(var + 1e-06)

    for ch in range(NC):
        for col in (0, 1):
            arrived(gb[col * NC + ch].at[pl.ds(0, 63)], send_sem.at[col, ch])
    for n, buf in ((0, nbuf), (1, mbuf)):
        for k in range(3):
            arrived(buf.at[0], ag_send.at[n, k])
    for g in range(GA):
        arrived(s1a.at[g], ea_send.at[0, g])
        arrived(s2a.at[g], ea_send.at[1, g])
    for g in range(GF):
        arrived(s1f.at[g], ef_send.at[0, g])
        arrived(s2f.at[g], ef_send.at[1, g])
    arrived(ra.at[pl.ds(0, 15)], rw_send.at[0])
    arrived(rb.at[pl.ds(0, 15)], rw_send.at[1])


def layer(pos, lengths, rel_bias, hidden, gains, srcs):
    hbm = pl.BlockSpec(memory_space=pl.ANY)
    vm = pl.BlockSpec(memory_space=pltpu.VMEM)
    sm = pl.BlockSpec(memory_space=pltpu.SMEM)
    dma = pltpu.SemaphoreType.DMA
    v = pltpu.VMEM
    scratch = [v((64, 32, n), BF) for _ in range(2) for n in CH]
    scratch += [
        v((4, ROWS, D), BF), v((4, ROWS, D), BF), v((8, 3, ROWS, ROWS), F32), v((2, LEN, 768), BF),
        v((LEN, 512), BF), v((LEN, 1280), BF), v((4, ROWS, D), F32), v((ROWS, D), F32),
    ]
    for g in (GA, GF):
        w = D // g
        scratch += [v((g, 2, ROWS, w), BF), v((g, 2, ROWS, w), BF), v((g, ROWS, w), BF), v((g, ROWS, w), BF)]
    scratch += [v((16, 8, 128), F32), v((16, 8, 128), F32)]
    scratch += [dma((2, NC)), dma((2, NC, 7)), dma((2, NC)), dma((2, 3)), dma((2, 3))]
    scratch += [dma((2, GA)), dma((2, GA)), dma((2, GF)), dma((2, GF)), dma((2,)), dma((2,))]
    return pl.pallas_call(
        layer_kernel,
        out_shape=(jax.ShapeDtypeStruct((ROWS, D), F32), jax.ShapeDtypeStruct((8, 128), F32)),
        in_specs=[sm, sm, sm, vm, vm] + [hbm] * (2 * NC),
        out_specs=(vm, vm),
        scratch_shapes=scratch,
        compiler_params=pltpu.CompilerParams(
            collective_id=0, has_side_effects=True, vmem_limit_bytes=67043328
        ),
        name="layer",
    )(pos, lengths, rel_bias, hidden, gains, *srcs)


def local(
    hidden_states, lengths, shard_order, gain_attn, w_query, w_key, w_value, w_out, rel_bias, gain_ff,
    w_gate, w_up, w_down, gain_final, w_reward,
):
    ids = jnp.arange(64, dtype=jnp.int32)
    inverse = jnp.sum(ids[:, None] * (shard_order[:, None] == ids[None, :]).astype(jnp.int32), axis=0)
    zs, xs, ys = inverse // 16, (inverse // 4) % 4, inverse % 4
    pos = jnp.stack([ys * 16 + xs * 4 + zs, xs * 16 + ys * 4 + zs])
    gains = jnp.stack([gain_attn, gain_ff, gain_final, w_reward])
    out_t, down_t = w_out.T, w_down.T
    srcs = []
    for col in (0, 1):
        a = slice(col * 256, col * 256 + 256)
        big = (w_gate, w_up)[col]
        srcs += [
            jnp.concatenate([w_query[:, a], w_key[:, a], w_value[:, a]], axis=1), out_t[:, a],
            big[:, :768], big[:, 768:], down_t[:, col * 640 : col * 640 + 640],
        ]
    rows, normalized = layer(pos, lengths, rel_bias, hidden_states, gains, srcs)
    return rows, normalized[0, :1]


def solution(mesh):
    placed = (
        P(("dp", "tensor"), None), P("dp"), P(), P(), P("dp", "tensor"), P("dp", "tensor"), P("dp", "tensor"),
        P("tensor", "dp"), P(None, "tensor"), P(), P("dp", "tensor"), P("dp", "tensor"), P("tensor", "dp"),
        P(), P(),
    )
    return jax.shard_map(
        local, mesh=mesh, in_specs=placed, out_specs=(P(("dp", "tensor"), None), P("dp")), check_vma=False
    )
```

time: 1600 us -> 250 us (0.16)
  waiting for transfers between devices: 1250 us -> 0 us
  Pallas kernels: 0 us -> 234 us
  starting transfers between devices: 108 us -> 0 us
  local copies, waits for them, and re-layouts: 95.1 us -> 10.3 us
  matrix products: 63.7 us -> 0 us
  blocking collectives: 44.2 us -> 0 us
  between operations: 18.8 us -> 1.35 us
    all_gather x4 -> x0, waiting for transfers between devices: 1050 us -> none  [the longest x2 483 us: in_one_piece(): lax.all_gather(both, axis, axis=dim, tiled=True)]
    pallas_call x0 -> x1, Pallas kernels: none -> 234 us  [layer(): pl.pallas_call(layer_kernel, out_shape=(jax.ShapeDtypeStruct((ROWS, D), F...]
    all_to_all x4 -> x0, starting transfers between devices: 108 us -> none  [the longest x1 86.6 us: sent_and_summed(): parts = lax.all_to_all(cut_along(array, dim, peers), axis, 0, 0, tiled=True)]
    all_to_all x4 -> x0, waiting for transfers between devices: 98.9 us -> none  [the longest x3 62.2 us: from_everyone(): lax.all_to_all(jnp.broadcast_to(array[None], (peers, *array.shape)), axis...]
    reduce_scatter x1 -> x0, waiting for transfers between devices: 98.7 us -> none  [local(): lax.psum_scatter(feed_partial, 'tensor', scatter_dimension=0, tiled=True)]
    dot_general x24 -> x0, matrix products: 63.7 us -> none  [the longest x4 19 us: contract(): return jnp.dot(source, portion, preferred_element_type=jnp.float32)]
    all_to_all x1 -> x0, blocking collectives: 44.2 us -> none  [from_everyone(): lax.all_to_all(jnp.broadcast_to(array[None], (peers, *array.shape)), axis...]
    reshape x17 -> x0, local copies, waits for them, and re-layouts: 34.8 us -> none  [the longest x8 23.2 us: head_step(): jnp.tile(head_offsets, LEN)[:LEN * (span - 1)].reshape(LEN, span - 1)]
  transfers between devices with their start and end apart: 9 -> 0, of which waited for: 9 -> 0; matrix products, arithmetic and copies ran while one was open for 8% -> 0% of each run, Pallas kernels for 0% -> 0%
where the time goes in v2:
time: 250 us
  Pallas kernels  234 us (94%)
  local copies, waits for them, and re-layouts  10.3 us (4%)
  other arithmetic  3.39 us (1%)
    pallas_call x1, Pallas kernels, layer(): pl.pallas_call(layer_kernel, out_shape=(jax.ShapeDtypeStruct((ROWS, D), F...  234 us
    unnamed x16, local copies, waits for them, and re-layouts  5.46 us

profile of v2, /device:TPU:1, one launch (start us, length us, event | category | flops | bytes accessed | tf_op | source)
XLA Modules:
  0.0 249.5 jit_solution(8645559473113272507)
XLA Ops:
  0.6 0.0 copy-start
  1.3 0.0 copy-start.1
  1.3 0.8 select_reduce_fusion
  2.1 0.6 pad_add_fusion.refs_0_
  2.7 1.4 copy.18.refs_2_
  4.1 1.4 pad_maximum_fusion.2.refs_4_
  5.4 0.0 copy-done
  5.5 0.6 slice.50.refs_8_
  6.1 0.0 copy-done.1
  6.1 0.0 copy-start.3
  6.1 0.6 slice.57.refs_13_
  6.7 0.2 copy-done.3
  6.8 0.8 copy-done.4
  7.6 0.8 copy-done.5
  8.4 0.6 pad_maximum_fusion
  9.0 0.1 copy-done.6
  9.1 0.6 fusion.2
  9.7 0.6 slice.49.refs_7_
  10.3 0.6 slice.56.refs_12_
  10.9 0.0 copy-done.2
  10.9 0.6 fusion.1
  11.6 234.4 %layer.1 = (f32[128,2048]{1,0:T(8,128)}, f32[8,128]{1,0:T(8,128)}) custom-call(s32[2,64]{1,0:T(2,128)} %pad_add_fusion.refs_0_, s32[1]{0:T(128)S(6)} %copy.20.refs_1_, f32[32,8]{1,0:T(8,128)} %copy.18.refs_2_, f32[128,2048]{1,0:T(8,128)} %refs_3_.1, f32[4,2048]{1,0:T(4,128)} %pad_maximum_fusion.2.refs_4_, bf16[32,768]{1,0:T(8,128)(2,1)} %get-tuple-element.18.refs_5_, ...), custom_call_target="tpu_custom_call" | custom-call | tf_op jit(solution)/shard_map/layer/pallas_call | solution.py:364
  246.0 1.2 slice.59
  247.2 2.3 copy.21
  (8 shorter events, 0.0 us)
Async XLA Ops:
  0.6 4.8 %copy-start = (bf16[32,1280]{1,0:T(8,128)(2,1)S(1)}, bf16[32,1280]{1,0:T(8,128)(2,1)}, u32[]{:S(2)}) copy-start(bf16[32,1280]{1,0:T(8,128)(2,1)} %param.25) | copy-start | bytes 245764
  1.3 4.7 %copy-start.1 = (bf16[32,1280]{1,0:T(8,128)(2,1)S(1)}, bf16[32,1280]{1,0:T(8,128)(2,1)}, u32[]{:S(2)}) copy-start(bf16[32,1280]{1,0:T(8,128)(2,1)} %param.26) | copy-start | bytes 245764
  6.1 0.8 copy-start.3
  6.8 0.8 copy-start.4
  7.6 0.8 copy-start.5
  8.4 0.8 copy-start.6
  9.7 1.2 copy-start.2

commit v3 on v2

--- a/solution.py
+++ b/solution.py
@@ -12,7 +12,7 @@
 MESH = pl.DeviceIdType.MESH
 BF = jnp.bfloat16
 F32 = jnp.float32
-CH = (768, 256, 768, 512, 640)
+CH = (768, 256, 768, 512, 384, 256)
 NC = len(CH)
 GA, GF = 2, 4
 bucket_edges = (12, 16, 23, 32, 46, 64, 91)
@@ -37,8 +37,7 @@
 
 
 def layer_kernel(*refs):
-    (pos, length_ref, rel, hidden, gains), refs = refs[:5], refs[5:]
-    src, refs = refs[: 2 * NC], refs[2 * NC :]
+    (pos, length_ref, rel, hidden, gains, wq, wk, wv, wgate, wup, wt), refs = refs[:11], refs[11:]
     (out, norm_out), refs = refs[:2], refs[2:]
     gb, refs = refs[: 2 * NC], refs[2 * NC :]
     (nbuf, mbuf, bias, qkv, ctx, act, part, mid, s1a, r1a, s2a, r2a, s1f, r1f, s2f, r2f, ra, rb) = refs[:18]
@@ -60,13 +59,35 @@
         i = (plane + k) % 16
         return did(z, i // 4, i % 4, h, c)
 
+    base = (y * 16 + x * 4, x * 16 + y * 4)
+
+    def pieces(col, ch):
+        a = slice(col * 256, col * 256 + 256)
+        big = (wgate, wup)[col]
+        if ch == 0:
+            return [wq.at[:, a], wk.at[:, a], wv.at[:, a]]
+        if ch == 1:
+            return [wt.at[:, a]]
+        if ch in (2, 3):
+            return [big.at[:, slice(0, 768) if ch == 2 else slice(768, 1280)]]
+        at = 512 + col * 640
+        return [wt.at[:, slice(at, at + 384) if ch == 4 else slice(at + 384, at + 640)]]
+
+    for ch in range(NC):
+        for col in (0, 1):
+            at = 0
+            for piece in pieces(col, ch):
+                n = piece.shape[1]
+                here = gb[col * NC + ch].at[base[col] + z, :, at : at + n]
+                pltpu.make_async_copy(piece, here, loc_sem.at[col, ch]).start()
+                at += n
+
     barrier = pltpu.get_barrier_semaphore()
     for k in range(1, 16):
         pl.semaphore_signal(barrier, inc=1, device_id=line_peer(k), device_id_type=MESH)
         pl.semaphore_signal(barrier, inc=1, device_id=plane_peer(k), device_id_type=MESH)
     pl.semaphore_wait(barrier, 30)
 
-    base = (y * 16 + x * 4, x * 16 + y * 4)
     ring1, ring2 = (x, y), (y, x)
 
     def remote(s, d, ss, rs, dev):
@@ -96,21 +117,16 @@
         arrived(gb[col * NC + ch].at[pl.ds(0, size)], recv_sem.at[col, ch, slot])
 
     def level(col, ch, lv):
-        g, s = gb[col * NC + ch], src[col * NC + ch]
         if lv == 0:
-            mine = base[col] + z
-            pltpu.make_async_copy(s, g.at[mine], loc_sem.at[col, ch]).start()
-            for k in (1, 2, 3):
+            mine = gb[col * NC + ch].at[base[col] + z]
+            arrived(mine, loc_sem.at[col, ch])
+            for k in (1, 3, 2):
                 remote(
-                    s, g.at[mine], send_sem.at[col, ch], recv_sem.at[col, ch, 0], did((z + k) % 4, x, y, h, c)
+                    mine, mine, send_sem.at[col, ch], recv_sem.at[col, ch, 0], did((z + k) % 4, x, y, h, c)
                 ).start()
         elif lv in (1, 3):
             ph = 1 if lv == 1 else 2
-            if ph == 1:
-                pltpu.make_async_copy(s, g.at[0], loc_sem.at[col, ch]).wait()
-                came(col, ch, 0, 3)
-            else:
-                came(col, ch, 3, 4)
+            came(col, ch, 0 if ph == 1 else 3, 3 if ph == 1 else 4)
             size, b = (4, 1) if ph == 1 else (16, 4)
             for j, k in ((0, 1), (1, 3)):
                 send(col, ch, section(col, ph, 0), size, b + j, ring_peer(col, ph, k))
@@ -125,11 +141,10 @@
         else:
             came(col, ch, 6, 16)
 
-    def wave(t):
-        for ch in range(NC):
-            if 0 <= t - ch <= 5:
-                for col in (0, 1):
-                    level(col, ch, t - ch)
+    def events(*steps):
+        for ch, lv in steps:
+            for col in (0, 1):
+                level(col, ch, lv)
 
     def spread(buf, n):
         to_sib = remote(buf.at[me], buf.at[me], ag_send.at[n, 0], ag_recv.at[n, 0], sib)
@@ -145,31 +160,32 @@
         arrived(buf.at[0], ag_recv.at[n, 0])
         arrived(buf.at[0], ag_recv.at[n, 2])
 
-    def to_sibling(g, width, s1, r1, ss, rs):
+    def to_sibling(which, g, width, s1, r1, ss, rs):
         cols = slice(g * width, (g + 1) * width)
-        s1[g, 0] = part[i_sib, :, cols].astype(BF)
-        s1[g, 1] = part[i_farsib, :, cols].astype(BF)
-        remote(s1.at[g], r1.at[g], ss.at[0, g], rs.at[0, g], sib).start()
+        s1[which, g] = part[(i_sib, i_farsib)[which], :, cols].astype(BF)
+        remote(s1.at[which, g], r1.at[which, g], ss.at[which, g], rs.at[which, g], sib).start()
 
     def to_far(g, width, r1, s2, r2, ss, rs):
         cols = slice(g * width, (g + 1) * width)
-        arrived(r1.at[g], rs.at[0, g])
-        s2[g] = (part[i_far, :, cols] + r1[g, 1].astype(F32)).astype(BF)
-        remote(s2.at[g], r2.at[g], ss.at[1, g], rs.at[1, g], far).start()
+        arrived(r1.at[1, g], rs.at[1, g])
+        s2[g] = (part[i_far, :, cols] + r1[1, g].astype(F32)).astype(BF)
+        remote(s2.at[g], r2.at[g], ss.at[2, g], rs.at[2, g], far).start()
 
     def total(g, width, r1, r2, rs):
         cols = slice(g * width, (g + 1) * width)
-        arrived(r2.at[g], rs.at[1, g])
-        return part[me, :, cols] + r1[g, 0].astype(F32) + r2[g].astype(F32)
+        arrived(r1.at[0, g], rs.at[0, g])
+        arrived(r2.at[g], rs.at[2, g])
+        return part[me, :, cols] + r1[0, g].astype(F32) + r2[g].astype(F32)
 
     def blocks(col, ch, first, count, cols):
         g = gb[col * NC + ch]
         return jnp.concatenate([g[pos[col, first + b], :, cols] for b in range(count)], axis=0)
 
-    wave(0)
+    events((1, 0), (0, 0))
     nbuf[me] = rms(hidden[...], gains[0:1]).astype(BF)
+    events((1, 1), (2, 0), (1, 2), (1, 3), (0, 1), (0, 2), (1, 4), (2, 1))
     spread(nbuf, 0)
-    wave(1)
+    events((0, 3))
 
     row = lax.broadcasted_iota(jnp.int32, (ROWS, ROWS), 0)
     lane = lax.broadcasted_iota(jnp.int32, (ROWS, ROWS), 1)
@@ -189,12 +205,11 @@
         return 0
 
     lax.fori_loop(0, 8, bias_tile, 0)
-    wave(2)
-    wave(3)
+    events((3, 0), (2, 2), (0, 4), (2, 3))
     pass_on(nbuf, 0)
-    wave(4)
+    events((4, 0), (5, 0), (3, 1))
     spread_end(nbuf, 0)
-    wave(5)
+    events((0, 5))
 
     for col in (0, 1):
         def qkv_tile(i, _):
@@ -237,64 +252,89 @@
                 pr = (e * (1.0 / jnp.sum(e, axis=-1, keepdims=True))).astype(BF)
                 got.append(jnp.dot(pr, values, preferred_element_type=F32))
             c_cols = pl.ds(pl.multiple_of(p * 128, 128), 128)
-            ctx[qt * ROWS : (qt + 1) * ROWS, c_cols] = jnp.where(lane_q < 64, got[0], got[1]).astype(BF)
+            ctx[qt, :, c_cols] = jnp.where(lane_q < 64, got[0], got[1]).astype(BF)
         return 0
 
-    lax.fori_loop(0, 2, heads, 0)
-    wave(6)
-    lax.fori_loop(2, 4, heads, 0)
-
-    def out_tile(i, _):
+    lax.fori_loop(0, 4, heads, 0)
+    events((1, 5), (2, 4), (3, 2), (4, 1), (5, 1))
+
+    rows_far, rows_own = pl.ds((1 - h) * 2, 2), pl.ds(h * 2, 2)
+
+    def out_tile(rows, i):
         cols = pl.ds(pl.multiple_of(i * 256, 256), 256)
-        all_ = slice(0, 256)
-        s = nt(ctx[:, :256], blocks(0, 1, i * 8, 8, all_)) + nt(ctx[:, 256:], blocks(1, 1, i * 8, 8, all_))
-        part[:, :, cols] = s.reshape(4, ROWS, 256)
+        c_ = ctx[rows].reshape(256, 512)
+        s = nt(c_[:, :256], blocks(0, 1, i * 8, 8, slice(0, 256)))
+        s = s + nt(c_[:, 256:], blocks(1, 1, i * 8, 8, slice(0, 256)))
+        part[rows, :, cols] = s.reshape(2, ROWS, 256)
         return 0
 
     wa = D // GA
+    na = 8 // GA
+    xa = (s1a, r1a, ea_send, ea_recv)
     for g in range(GA):
-        lax.fori_loop(g * (8 // GA), (g + 1) * (8 // GA), out_tile, 0)
-        to_sibling(g, wa, s1a, r1a, ea_send, ea_recv)
+        lax.fori_loop(g * na, (g + 1) * na, lambda i, _: out_tile(rows_far, i), 0)
+        to_sibling(1, g, wa, *xa)
     for g in range(GA):
+        lax.fori_loop(g * na, (g + 1) * na, lambda i, _: out_tile(rows_own, i), 0)
+        to_sibling(0, g, wa, *xa)
         to_far(g, wa, r1a, s2a, r2a, ea_send, ea_recv)
-    wave(7)
+    events((3, 3), (2, 5), (4, 2), (5, 2))
     for g in range(GA):
         cols = slice(g * wa, (g + 1) * wa)
         mid[:, cols] = hidden[:, cols] + total(g, wa, r1a, r2a, ea_recv)
     mbuf[me] = rms(mid[...], gains[1:2]).astype(BF)
     spread(mbuf, 1)
-    wave(8)
-    pass_on(mbuf, 1)
-    spread_end(mbuf, 1)
-
-    def feed_tile(ch, i, at):
+    events((3, 4), (4, 3), (5, 3))
+    arrived(mbuf.at[0], ag_recv.at[1, 0])
+
+    def feed_tile(rows, ch, i, at):
         cols = pl.ds(pl.multiple_of(i * 256, 256), 256)
-        lhs = mbuf[...].reshape(LEN, D)
+        lhs = mbuf[rows].reshape(256, D)
         gate = jnp.dot(lhs, blocks(0, ch, 0, 64, cols), preferred_element_type=F32)
         up = jnp.dot(lhs, blocks(1, ch, 0, 64, cols), preferred_element_type=F32)
-        act[:, pl.ds(pl.multiple_of(at + i * 256, 256), 256)] = (
-            jax.nn.gelu(gate, approximate=True) * up
-        ).astype(BF)
+        a = (jax.nn.gelu(gate, approximate=True) * up).astype(BF)
+        act[rows, :, pl.ds(pl.multiple_of(at + i * 256, 256), 256)] = a.reshape(2, ROWS, 256)
         return 0
 
-    lax.fori_loop(0, 3, lambda i, _: feed_tile(2, i, 0), 0)
-    lax.fori_loop(0, 2, lambda i, _: feed_tile(3, i, 768), 0)
-    wave(9)
-
-    def down_tile(i, _):
+    def feed_a(rows):
+        lax.fori_loop(0, 3, lambda i, _: feed_tile(rows, 2, i, 0), 0)
+
+    def feed_b(rows):
+        lax.fori_loop(0, 2, lambda i, _: feed_tile(rows, 3, i, 768), 0)
+
+    feed_a(rows_own)
+    events((3, 5))
+    feed_b(rows_own)
+    events((4, 4), (5, 4))
+    pass_on(mbuf, 1)
+    arrived(mbuf.at[0], ag_recv.at[1, 2])
+    feed_a(rows_far)
+    feed_b(rows_far)
+    events((4, 5), (5, 5))
+
+    def down_tile(rows, i):
         cols = pl.ds(pl.multiple_of(i * 256, 256), 256)
-        all_ = slice(0, 640)
-        s = nt(act[:, :640], blocks(0, 4, i * 8, 8, all_)) + nt(act[:, 640:], blocks(1, 4, i * 8, 8, all_))
-        part[:, :, cols] = s.reshape(4, ROWS, 256)
+        s = None
+        for col, ch, at in ((0, 4, 0), (0, 5, 384), (1, 4, 640), (1, 5, 1024)):
+            n = CH[ch]
+            t = nt(act[rows, :, at : at + n].reshape(256, n), blocks(col, ch, i * 8, 8, slice(0, n)))
+            s = t if s is None else s + t
+        part[rows, :, cols] = s.reshape(2, ROWS, 256)
         return 0
 
     wf = D // GF
+    nf = 8 // GF
+    xf = (s1f, r1f, ef_send, ef_recv)
     for g in range(GF):
-        lax.fori_loop(g * (8 // GF), (g + 1) * (8 // GF), down_tile, 0)
-        to_sibling(g, wf, s1f, r1f, ef_send, ef_recv)
+        lax.fori_loop(g * nf, (g + 1) * nf, lambda i, _: down_tile(rows_far, i), 0)
+        to_sibling(1, g, wf, *xf)
         if g > 0:
             to_far(g - 1, wf, r1f, s2f, r2f, ef_send, ef_recv)
-    to_far(GF - 1, wf, r1f, s2f, r2f, ef_send, ef_recv)
+    for g in range(GF):
+        lax.fori_loop(g * nf, (g + 1) * nf, lambda i, _: down_tile(rows_own, i), 0)
+        to_sibling(0, g, wf, *xf)
+        if g == 0:
+            to_far(GF - 1, wf, r1f, s2f, r2f, ef_send, ef_recv)
     square = jnp.zeros((ROWS, 1), F32)
     dot = jnp.zeros((ROWS, 1), F32)
     for g in range(GF):
@@ -334,17 +374,16 @@
     for n, buf in ((0, nbuf), (1, mbuf)):
         for k in range(3):
             arrived(buf.at[0], ag_send.at[n, k])
-    for g in range(GA):
-        arrived(s1a.at[g], ea_send.at[0, g])
-        arrived(s2a.at[g], ea_send.at[1, g])
-    for g in range(GF):
-        arrived(s1f.at[g], ef_send.at[0, g])
-        arrived(s2f.at[g], ef_send.at[1, g])
+    for n, s1, s2, ss in ((GA, s1a, s2a, ea_send), (GF, s1f, s2f, ef_send)):
+        for g in range(n):
+            arrived(s1.at[0, g], ss.at[0, g])
+            arrived(s1.at[1, g], ss.at[1, g])
+            arrived(s2.at[g], ss.at[2, g])
     arrived(ra.at[pl.ds(0, 15)], rw_send.at[0])
     arrived(rb.at[pl.ds(0, 15)], rw_send.at[1])
 
 
-def layer(pos, lengths, rel_bias, hidden, gains, srcs):
+def layer(pos, lengths, rel_bias, hidden, gains, *weights):
     hbm = pl.BlockSpec(memory_space=pl.ANY)
     vm = pl.BlockSpec(memory_space=pltpu.VMEM)
     sm = pl.BlockSpec(memory_space=pltpu.SMEM)
@@ -353,25 +392,25 @@
     scratch = [v((64, 32, n), BF) for _ in range(2) for n in CH]
     scratch += [
         v((4, ROWS, D), BF), v((4, ROWS, D), BF), v((8, 3, ROWS, ROWS), F32), v((2, LEN, 768), BF),
-        v((LEN, 512), BF), v((LEN, 1280), BF), v((4, ROWS, D), F32), v((ROWS, D), F32),
+        v((4, ROWS, 512), BF), v((4, ROWS, 1280), BF), v((4, ROWS, D), F32), v((ROWS, D), F32),
     ]
     for g in (GA, GF):
         w = D // g
-        scratch += [v((g, 2, ROWS, w), BF), v((g, 2, ROWS, w), BF), v((g, ROWS, w), BF), v((g, ROWS, w), BF)]
+        scratch += [v((2, g, ROWS, w), BF), v((2, g, ROWS, w), BF), v((g, ROWS, w), BF), v((g, ROWS, w), BF)]
     scratch += [v((16, 8, 128), F32), v((16, 8, 128), F32)]
     scratch += [dma((2, NC)), dma((2, NC, 7)), dma((2, NC)), dma((2, 3)), dma((2, 3))]
-    scratch += [dma((2, GA)), dma((2, GA)), dma((2, GF)), dma((2, GF)), dma((2,)), dma((2,))]
+    scratch += [dma((3, GA)), dma((3, GA)), dma((3, GF)), dma((3, GF)), dma((2,)), dma((2,))]
     return pl.pallas_call(
         layer_kernel,
         out_shape=(jax.ShapeDtypeStruct((ROWS, D), F32), jax.ShapeDtypeStruct((8, 128), F32)),
-        in_specs=[sm, sm, sm, vm, vm] + [hbm] * (2 * NC),
+        in_specs=[sm, sm, sm, vm, vm] + [hbm] * 6,
         out_specs=(vm, vm),
         scratch_shapes=scratch,
         compiler_params=pltpu.CompilerParams(
             collective_id=0, has_side_effects=True, vmem_limit_bytes=67043328
         ),
         name="layer",
-    )(pos, lengths, rel_bias, hidden, gains, *srcs)
+    )(pos, lengths, rel_bias, hidden, gains, *weights)
 
 
 def local(
@@ -383,16 +422,10 @@
     zs, xs, ys = inverse // 16, (inverse // 4) % 4, inverse % 4
     pos = jnp.stack([ys * 16 + xs * 4 + zs, xs * 16 + ys * 4 + zs])
     gains = jnp.stack([gain_attn, gain_ff, gain_final, w_reward])
-    out_t, down_t = w_out.T, w_down.T
-    srcs = []
-    for col in (0, 1):
-        a = slice(col * 256, col * 256 + 256)
-        big = (w_gate, w_up)[col]
-        srcs += [
-            jnp.concatenate([w_query[:, a], w_key[:, a], w_value[:, a]], axis=1), out_t[:, a],
-            big[:, :768], big[:, 768:], down_t[:, col * 640 : col * 640 + 640],
-        ]
-    rows, normalized = layer(pos, lengths, rel_bias, hidden_states, gains, srcs)
+    wt = jnp.concatenate([w_out, w_down], axis=0).T
+    rows, normalized = layer(
+        pos, lengths, rel_bias, hidden_states, gains, w_query, w_key, w_value, w_gate, w_up, wt
+    )
     return rows, normalized[0, :1]
 
 

time: 250 us -> 198 us (0.79)
  Pallas kernels: 234 us -> 187 us
  local copies, waits for them, and re-layouts: 10.3 us -> 4.84 us
    pallas_call x1, Pallas kernels: 234 us -> 187 us  [layer(): pl.pallas_call(layer_kernel, out_shape=(jax.ShapeDtypeStruct((ROWS, D), F...]
    slice x9 -> x0, local copies, waits for them, and re-layouts: 3.69 us -> none  [the longest x2 1.23 us: local(): big[:, :768]]
    unnamed x16 -> x4, local copies, waits for them, and re-layouts: 5.46 us -> 3.66 us
where the time goes in v3:
time: 198 us
  Pallas kernels  187 us (94%)
  local copies, waits for them, and re-layouts  4.84 us (2%)
  other arithmetic  4.17 us (2%)
    pallas_call x1, Pallas kernels, layer(): pl.pallas_call(layer_kernel, out_shape=(jax.ShapeDtypeStruct((ROWS, D), F...  187 us

profile of v3, /device:TPU:1, one launch (start us, length us, event | category | flops | bytes accessed | tf_op | source)
XLA Modules:
  0.0 197.6 jit_solution(5881155205548919870)
XLA Ops:
  0.6 0.0 copy-start
  1.3 0.7 select_reduce_fusion
  2.1 0.6 pad_add_fusion.refs_0_
  2.7 1.4 copy.18.refs_2_
  4.0 1.4 pad_maximum_fusion.refs_4_
  5.4 0.0 copy-done
  5.4 1.4 maximum_bitcast_fusion.refs_10_
  6.9 187.2 %layer.1 = (f32[128,2048]{1,0:T(8,128)}, f32[8,128]{1,0:T(8,128)}) custom-call(s32[2,64]{1,0:T(2,128)} %pad_add_fusion.refs_0_, s32[1]{0:T(128)S(6)} %copy.20.refs_1_, f32[32,8]{1,0:T(8,128)} %copy.18.refs_2_, f32[128,2048]{1,0:T(8,128)} %refs_3_.1, f32[4,2048]{1,0:T(4,128)} %pad_maximum_fusion.refs_4_, bf16[32,512]{1,0:T(8,128)(2,1)} %refs_5_.1, ...), custom_call_target="tpu_custom_call" | custom-call | tf_op jit(solution)/shard_map/layer/pallas_call | solution.py:403
  194.1 1.2 slice.3
  195.3 2.3 %copy.21 = f32[128,2048]{1,0:T(8,128)} copy(f32[128,2048]{1,0:T(8,128)} %get-tuple-element.10) | data formatting | bytes 2097152
  (1 shorter events, 0.0 us)
Async XLA Ops:
  0.6 4.8 %copy-start = (bf16[1280,32]{0,1:T(8,128)(2,1)S(1)}, bf16[1280,32]{0,1:T(8,128)(2,1)}, u32[]{:S(2)}) copy-start(bf16[1280,32]{0,1:T(8,128)(2,1)} %param.27) | copy-start | bytes 245764

commit v4 on v3

--- a/solution.py
+++ b/solution.py
@@ -12,7 +12,7 @@
 MESH = pl.DeviceIdType.MESH
 BF = jnp.bfloat16
 F32 = jnp.float32
-CH = (768, 256, 768, 512, 384, 256)
+CH = ((32, 384), (32, 384), (32, 256), (32, 768), (32, 512), (16, 640), (16, 640))
 NC = len(CH)
 GA, GF = 2, 4
 bucket_edges = (12, 16, 23, 32, 46, 64, 91)
@@ -37,11 +37,13 @@
 
 
 def layer_kernel(*refs):
-    (pos, length_ref, rel, hidden, gains, wq, wk, wv, wgate, wup, wt), refs = refs[:11], refs[11:]
-    (out, norm_out), refs = refs[:2], refs[2:]
+    (pos, length_ref, rel, hidden, gain_attn, gain_ff, gain_final, w_reward), refs = refs[:8], refs[8:]
+    (wq, wk, wv, wgate, wup, wout, wdown), refs = refs[:7], refs[7:]
+    (out_hbm, norm_out), refs = refs[:2], refs[2:]
     gb, refs = refs[: 2 * NC], refs[2 * NC :]
     (nbuf, mbuf, bias, qkv, ctx, act, part, mid, s1a, r1a, s2a, r2a, s1f, r1f, s2f, r2f, ra, rb) = refs[:18]
-    send_sem, recv_sem, loc_sem, ag_send, ag_recv, ea_send, ea_recv, ef_send, ef_recv, rw_send, rw_recv = refs[18:]
+    (gain_t, gain_p, out), refs = refs[18:21], refs[21:]
+    send_sem, recv_sem, loc_sem, ag_send, ag_recv, ea_send, ea_recv, ef_send, ef_recv, rw_send, rw_recv, out_sem = refs
     z, x, y, h, c = coords()
     me = h * 2 + c
     sib, far = did(z, x, y, h, 1 - c), did(z, x, y, 1 - h, c)
@@ -62,16 +64,15 @@
     base = (y * 16 + x * 4, x * 16 + y * 4)
 
     def pieces(col, ch):
-        a = slice(col * 256, col * 256 + 256)
         big = (wgate, wup)[col]
-        if ch == 0:
-            return [wq.at[:, a], wk.at[:, a], wv.at[:, a]]
-        if ch == 1:
-            return [wt.at[:, a]]
-        if ch in (2, 3):
-            return [big.at[:, slice(0, 768) if ch == 2 else slice(768, 1280)]]
-        at = 512 + col * 640
-        return [wt.at[:, slice(at, at + 384) if ch == 4 else slice(at + 384, at + 640)]]
+        if ch in (0, 1):
+            at = col * 256 + ch * 128
+            return [w.at[:, at : at + 128] for w in (wq, wk, wv)]
+        if ch == 2:
+            return [wout.at[:, col * 256 : col * 256 + 256]]
+        if ch in (3, 4):
+            return [big.at[:, slice(0, 768) if ch == 3 else slice(768, 1280)]]
+        return [wdown.at[slice(0, 16) if ch == 5 else slice(16, 32), col * 640 : col * 640 + 640]]
 
     for ch in range(NC):
         for col in (0, 1):
@@ -177,15 +178,21 @@
         arrived(r2.at[g], rs.at[2, g])
         return part[me, :, cols] + r1[0, g].astype(F32) + r2[g].astype(F32)
 
-    def blocks(col, ch, first, count, cols):
+    def blocks(col, ch, first, count, cols, rows=slice(None)):
         g = gb[col * NC + ch]
-        return jnp.concatenate([g[pos[col, first + b], :, cols] for b in range(count)], axis=0)
-
-    events((1, 0), (0, 0))
-    nbuf[me] = rms(hidden[...], gains[0:1]).astype(BF)
-    events((1, 1), (2, 0), (1, 2), (1, 3), (0, 1), (0, 2), (1, 4), (2, 1))
-    spread(nbuf, 0)
-    events((0, 3))
+        return jnp.concatenate([g[pos[col, first + b], rows, cols] for b in range(count)], axis=0)
+
+    def pick(k):
+        i = lax.broadcasted_iota(jnp.int32, (256, 128), 0)
+        j = lax.broadcasted_iota(jnp.int32, (256, 128), 1)
+        return (i == (j // 16) * 32 + k * 16 + j % 16).astype(F32)
+
+    def halves_first(ref, put):
+        for k in (0, 1):
+            p = pick(k)
+            for v in range(8):
+                t = jnp.dot(ref[:, v * 256 : v * 256 + 256], p, precision=lax.Precision.HIGHEST, preferred_element_type=F32)
+                put(slice(k * 1024 + v * 128, k * 1024 + v * 128 + 128), t)
 
     row = lax.broadcasted_iota(jnp.int32, (ROWS, ROWS), 0)
     lane = lax.broadcasted_iota(jnp.int32, (ROWS, ROWS), 1)
@@ -200,42 +207,54 @@
             bucket = jnp.where(r > 0, 16, 0) + low
             tile = jnp.zeros((ROWS, ROWS), F32)
             for b in range(32):
-                tile = jnp.where(bucket == b, rel[b, n], tile)
+                tile = jnp.where(bucket == b, rel[n, b], tile)
             bias[n, o] = tile
         return 0
 
-    lax.fori_loop(0, 8, bias_tile, 0)
-    events((3, 0), (2, 2), (0, 4), (2, 3))
+    def bias_half():
+        lax.fori_loop(0, 4, bias_tile, 0)
+
+    pl.when(c == 1)(bias_half)
+    events((0, 0))
+    nbuf[me] = rms(hidden[...], gain_attn[...]).astype(BF)
+    events((0, 1), (1, 0), (2, 0), (0, 2), (1, 1))
+    spread(nbuf, 0)
+    events((3, 0), (0, 3), (1, 2))
+    pl.when(c == 0)(bias_half)
+    lax.fori_loop(4, 8, bias_tile, 0)
+
+    def put_mid(cols, t):
+        mid[:, cols] = t
+
+    def put_gain(cols, t):
+        gain_p[:, cols] = t
+
+    halves_first(hidden, put_mid)
+    gain_t[0:1] = gain_ff[...]
+    gain_t[1:2] = gain_final[...] * w_reward[...]
+    gain_t[2:8] = jnp.zeros((6, D), F32)
+    halves_first(gain_t, put_gain)
+    events((0, 4), (1, 3), (2, 1), (2, 2))
     pass_on(nbuf, 0)
-    events((4, 0), (5, 0), (3, 1))
+    events((3, 1))
     spread_end(nbuf, 0)
-    events((0, 5))
-
-    for col in (0, 1):
-        def qkv_tile(i, _):
-            cols = pl.ds(pl.multiple_of(i * 256, 256), 256)
-            w = blocks(col, 0, 0, 64, cols)
-            qkv[col, :, cols] = jnp.dot(
-                nbuf[...].reshape(LEN, D), w, preferred_element_type=F32
-            ).astype(BF)
-            return 0
-
-        lax.fori_loop(0, 3, qkv_tile, 0)
+    events((4, 0), (5, 0), (6, 0), (0, 5))
+
+    def project(ch):
+        for col in (0, 1):
+            w = blocks(col, ch, 0, 64, slice(0, 384))
+            t = jnp.dot(nbuf[...].reshape(LEN, D), w, preferred_element_type=F32)
+            qkv[col * 2 + ch] = t.astype(BF)
 
     lane_q = lax.broadcasted_iota(jnp.int32, (ROWS, 128), 1)
     key_pos = lax.broadcasted_iota(jnp.int32, (ROWS, LEN), 1)
     valid = key_pos < length
 
     def heads(p, _):
-        col = p // 2
-        at = (p % 2) * 128
-        q_cols = pl.ds(pl.multiple_of(at, 128), 128)
-        k_cols = pl.ds(pl.multiple_of(at + 256, 128), 128)
-        v_cols = pl.ds(pl.multiple_of(at + 512, 128), 128)
-        keys = qkv[col, :, k_cols]
-        values = qkv[col, :, v_cols]
+        keys = qkv[p, :, 128:256]
+        values = qkv[p, :, 256:384]
         for qt in range(4):
-            q = qkv[col, qt * ROWS : (qt + 1) * ROWS, q_cols]
+            q = qkv[p, qt * ROWS : (qt + 1) * ROWS, 0:128]
             got = []
             for hh in (0, 1):
                 n = p * 2 + hh
@@ -246,7 +265,7 @@
                     if abs(kt - qt) <= 1:
                         tiles.append(bias[n, kt - qt + 1])
                     else:
-                        tiles.append(jnp.full((ROWS, ROWS), rel[31 if kt > qt else 15, n], F32))
+                        tiles.append(jnp.full((ROWS, ROWS), rel[n, 31 if kt > qt else 15], F32))
                 s = jnp.where(valid, s + jnp.concatenate(tiles, axis=1), -1e30)
                 e = jnp.exp(s - jnp.max(s, axis=-1, keepdims=True))
                 pr = (e * (1.0 / jnp.sum(e, axis=-1, keepdims=True))).astype(BF)
@@ -255,97 +274,132 @@
             ctx[qt, :, c_cols] = jnp.where(lane_q < 64, got[0], got[1]).astype(BF)
         return 0
 
-    lax.fori_loop(0, 4, heads, 0)
-    events((1, 5), (2, 4), (3, 2), (4, 1), (5, 1))
+    def pair(i, _):
+        return heads((i % 2) * 2 + i // 2, 0)
+
+    project(0)
+    events((1, 4), (2, 3))
+    lax.fori_loop(0, 1, pair, 0)
+    events((3, 2))
+    lax.fori_loop(1, 2, pair, 0)
+    events((1, 5))
+    project(1)
+    lax.fori_loop(2, 3, pair, 0)
+    events((2, 4), (3, 3))
+    lax.fori_loop(3, 4, pair, 0)
+    events((4, 1), (2, 5))
 
     rows_far, rows_own = pl.ds((1 - h) * 2, 2), pl.ds(h * 2, 2)
 
-    def out_tile(rows, i):
-        cols = pl.ds(pl.multiple_of(i * 256, 256), 256)
+    def out_tile(rows, k, i):
+        cols = pl.ds(pl.multiple_of(k * 1024 + i * 256, 256), 256)
         c_ = ctx[rows].reshape(256, 512)
-        s = nt(c_[:, :256], blocks(0, 1, i * 8, 8, slice(0, 256)))
-        s = s + nt(c_[:, 256:], blocks(1, 1, i * 8, 8, slice(0, 256)))
+        r = slice(k * 16, k * 16 + 16)
+        s = nt(c_[:, :256], blocks(0, 2, i * 16, 16, slice(0, 256), r))
+        s = s + nt(c_[:, 256:], blocks(1, 2, i * 16, 16, slice(0, 256), r))
         part[rows, :, cols] = s.reshape(2, ROWS, 256)
         return 0
 
     wa = D // GA
-    na = 8 // GA
     xa = (s1a, r1a, ea_send, ea_recv)
     for g in range(GA):
-        lax.fori_loop(g * na, (g + 1) * na, lambda i, _: out_tile(rows_far, i), 0)
+        lax.fori_loop(0, 4, lambda i, _: out_tile(rows_far, g, i), 0)
         to_sibling(1, g, wa, *xa)
     for g in range(GA):
-        lax.fori_loop(g * na, (g + 1) * na, lambda i, _: out_tile(rows_own, i), 0)
+        lax.fori_loop(0, 4, lambda i, _: out_tile(rows_own, g, i), 0)
         to_sibling(0, g, wa, *xa)
         to_far(g, wa, r1a, s2a, r2a, ea_send, ea_recv)
-    events((3, 3), (2, 5), (4, 2), (5, 2))
+    events((5, 1), (6, 1), (4, 2), (3, 4), (5, 2), (6, 2), (4, 3), (5, 3))
     for g in range(GA):
         cols = slice(g * wa, (g + 1) * wa)
-        mid[:, cols] = hidden[:, cols] + total(g, wa, r1a, r2a, ea_recv)
-    mbuf[me] = rms(mid[...], gains[1:2]).astype(BF)
+        mid[:, cols] = mid[:, cols] + total(g, wa, r1a, r2a, ea_recv)
+    mbuf[me] = rms(mid[...], gain_p[0:1]).astype(BF)
     spread(mbuf, 1)
-    events((3, 4), (4, 3), (5, 3))
+    events((3, 5))
     arrived(mbuf.at[0], ag_recv.at[1, 0])
 
     def feed_tile(rows, ch, i, at):
         cols = pl.ds(pl.multiple_of(i * 256, 256), 256)
         lhs = mbuf[rows].reshape(256, D)
-        gate = jnp.dot(lhs, blocks(0, ch, 0, 64, cols), preferred_element_type=F32)
-        up = jnp.dot(lhs, blocks(1, ch, 0, 64, cols), preferred_element_type=F32)
+
+        def both(col):
+            return jnp.concatenate([blocks(col, ch, 0, 64, cols, slice(k, k + 16)) for k in (0, 16)], axis=0)
+
+        gate = jnp.dot(lhs, both(0), preferred_element_type=F32)
+        up = jnp.dot(lhs, both(1), preferred_element_type=F32)
         a = (jax.nn.gelu(gate, approximate=True) * up).astype(BF)
         act[rows, :, pl.ds(pl.multiple_of(at + i * 256, 256), 256)] = a.reshape(2, ROWS, 256)
         return 0
 
     def feed_a(rows):
-        lax.fori_loop(0, 3, lambda i, _: feed_tile(rows, 2, i, 0), 0)
+        lax.fori_loop(0, 3, lambda i, _: feed_tile(rows, 3, i, 0), 0)
 
     def feed_b(rows):
-        lax.fori_loop(0, 2, lambda i, _: feed_tile(rows, 3, i, 768), 0)
+        lax.fori_loop(0, 2, lambda i, _: feed_tile(rows, 4, i, 768), 0)
 
     feed_a(rows_own)
-    events((3, 5))
-    feed_b(rows_own)
-    events((4, 4), (5, 4))
+    events((4, 4), (5, 4), (6, 3))
     pass_on(mbuf, 1)
     arrived(mbuf.at[0], ag_recv.at[1, 2])
     feed_a(rows_far)
+    events((4, 5))
     feed_b(rows_far)
-    events((4, 5), (5, 5))
-
-    def down_tile(rows, i):
-        cols = pl.ds(pl.multiple_of(i * 256, 256), 256)
-        s = None
-        for col, ch, at in ((0, 4, 0), (0, 5, 384), (1, 4, 640), (1, 5, 1024)):
-            n = CH[ch]
-            t = nt(act[rows, :, at : at + n].reshape(256, n), blocks(col, ch, i * 8, 8, slice(0, n)))
-            s = t if s is None else s + t
+    events((5, 5))
+
+    def down_tile(rows, k, i):
+        cols = pl.ds(pl.multiple_of(k * 1024 + i * 256, 256), 256)
+        a = act[rows].reshape(256, 1280)
+        s = nt(a[:, :640], blocks(0, 5 + k, i * 16, 16, slice(0, 640)))
+        s = s + nt(a[:, 640:], blocks(1, 5 + k, i * 16, 16, slice(0, 640)))
         part[rows, :, cols] = s.reshape(2, ROWS, 256)
         return 0
 
     wf = D // GF
-    nf = 8 // GF
     xf = (s1f, r1f, ef_send, ef_recv)
-    for g in range(GF):
-        lax.fori_loop(g * nf, (g + 1) * nf, lambda i, _: down_tile(rows_far, i), 0)
+
+    def down_far(g):
+        lax.fori_loop((g % 2) * 2, (g % 2) * 2 + 2, lambda i, _: down_tile(rows_far, g // 2, i), 0)
         to_sibling(1, g, wf, *xf)
-        if g > 0:
-            to_far(g - 1, wf, r1f, s2f, r2f, ef_send, ef_recv)
-    for g in range(GF):
-        lax.fori_loop(g * nf, (g + 1) * nf, lambda i, _: down_tile(rows_own, i), 0)
+
+    def down_own(g):
+        lax.fori_loop((g % 2) * 2, (g % 2) * 2 + 2, lambda i, _: down_tile(rows_own, g // 2, i), 0)
         to_sibling(0, g, wf, *xf)
-        if g == 0:
-            to_far(GF - 1, wf, r1f, s2f, r2f, ef_send, ef_recv)
+
+    down_far(0)
+    down_far(1)
+    to_far(0, wf, r1f, s2f, r2f, ef_send, ef_recv)
+    to_far(1, wf, r1f, s2f, r2f, ef_send, ef_recv)
+    events((6, 4))
+    feed_b(rows_own)
+    down_own(0)
+    down_own(1)
+    events((6, 5))
+    down_far(2)
+    down_far(3)
+    to_far(2, wf, r1f, s2f, r2f, ef_send, ef_recv)
+    down_own(2)
+    to_far(3, wf, r1f, s2f, r2f, ef_send, ef_recv)
+    down_own(3)
     square = jnp.zeros((ROWS, 1), F32)
     dot = jnp.zeros((ROWS, 1), F32)
     for g in range(GF):
         cols = slice(g * wf, (g + 1) * wf)
         o = mid[:, cols] + total(g, wf, r1f, r2f, ef_recv)
-        out[:, cols] = o
+        p = pick(g // 2)
+        for q in range(4):
+            v = (g % 2) * 4 + q
+            t = lax.dot_general(o[:, q * 128 : q * 128 + 128], p, (((1,), (1,)), ((), ())),
+                                precision=lax.Precision.HIGHEST, preferred_element_type=F32)
+            to = slice(v * 256, v * 256 + 256)
+            out[:, to] = t if g < 2 else out[:, to] + t
         square = square + jnp.sum(o * o, axis=-1, keepdims=True)
-        dot = dot + jnp.sum(o * (gains[2:3, cols] * gains[3:4, cols]), axis=-1, keepdims=True)
+        dot = dot + jnp.sum(o * gain_p[1:2, cols], axis=-1, keepdims=True)
     score = dot * lax.rsqrt(square * (1.0 / D) + 1e-06)
     at_row = lax.broadcasted_iota(jnp.int32, (ROWS, 1), 0) + me * ROWS
     pooled = jnp.sum(jnp.where(at_row < length, score, 0.0), axis=0, keepdims=True)
+
+    result = pltpu.make_async_copy(out, out_hbm, out_sem)
+    result.start()
 
     ra[line] = jnp.broadcast_to(pooled / length.astype(F32), (8, 128))
     copies = []
@@ -366,7 +420,7 @@
     mean = jnp.sum(every, axis=0, keepdims=True) * (1.0 / 64)
     off = jnp.where((sub < 4)[None], rb[...] - mean[None], 0.0)
     var = jnp.sum(jnp.sum(off * off, axis=0), axis=0, keepdims=True) * (1.0 / 64)
-    norm_out[...] = (own - mean) / jnp.sqrt(var + 1e-06)
+    norm_out[...] = ((own - mean) / jnp.sqrt(var + 1e-06))[0:1, 0:1]
 
     for ch in range(NC):
         for col in (0, 1):
@@ -381,36 +435,37 @@
             arrived(s2.at[g], ss.at[2, g])
     arrived(ra.at[pl.ds(0, 15)], rw_send.at[0])
     arrived(rb.at[pl.ds(0, 15)], rw_send.at[1])
-
-
-def layer(pos, lengths, rel_bias, hidden, gains, *weights):
+    result.wait()
+
+
+def layer(pos, lengths, rel_bias, hidden, *arrays):
     hbm = pl.BlockSpec(memory_space=pl.ANY)
     vm = pl.BlockSpec(memory_space=pltpu.VMEM)
     sm = pl.BlockSpec(memory_space=pltpu.SMEM)
     dma = pltpu.SemaphoreType.DMA
     v = pltpu.VMEM
-    scratch = [v((64, 32, n), BF) for _ in range(2) for n in CH]
+    scratch = [v((64, r, n), BF) for _ in range(2) for r, n in CH]
     scratch += [
-        v((4, ROWS, D), BF), v((4, ROWS, D), BF), v((8, 3, ROWS, ROWS), F32), v((2, LEN, 768), BF),
+        v((4, ROWS, D), BF), v((4, ROWS, D), BF), v((8, 3, ROWS, ROWS), F32), v((4, LEN, 384), BF),
         v((4, ROWS, 512), BF), v((4, ROWS, 1280), BF), v((4, ROWS, D), F32), v((ROWS, D), F32),
     ]
     for g in (GA, GF):
         w = D // g
         scratch += [v((2, g, ROWS, w), BF), v((2, g, ROWS, w), BF), v((g, ROWS, w), BF), v((g, ROWS, w), BF)]
-    scratch += [v((16, 8, 128), F32), v((16, 8, 128), F32)]
+    scratch += [v((16, 8, 128), F32), v((16, 8, 128), F32), v((8, D), F32), v((8, D), F32), v((ROWS, D), F32)]
     scratch += [dma((2, NC)), dma((2, NC, 7)), dma((2, NC)), dma((2, 3)), dma((2, 3))]
-    scratch += [dma((3, GA)), dma((3, GA)), dma((3, GF)), dma((3, GF)), dma((2,)), dma((2,))]
+    scratch += [dma((3, GA)), dma((3, GA)), dma((3, GF)), dma((3, GF)), dma((2,)), dma((2,)), dma]
     return pl.pallas_call(
         layer_kernel,
-        out_shape=(jax.ShapeDtypeStruct((ROWS, D), F32), jax.ShapeDtypeStruct((8, 128), F32)),
-        in_specs=[sm, sm, sm, vm, vm] + [hbm] * 6,
-        out_specs=(vm, vm),
+        out_shape=(jax.ShapeDtypeStruct((ROWS, D), F32), jax.ShapeDtypeStruct((1, 1), F32)),
+        in_specs=[sm, sm, sm] + [vm] * 5 + [hbm] * 7,
+        out_specs=(hbm, vm),
         scratch_shapes=scratch,
         compiler_params=pltpu.CompilerParams(
-            collective_id=0, has_side_effects=True, vmem_limit_bytes=67043328
+            collective_id=0, has_side_effects=True, vmem_limit_bytes=56 << 20
         ),
         name="layer",
-    )(pos, lengths, rel_bias, hidden, gains, *weights)
+    )(pos, lengths, rel_bias, hidden, *arrays)
 
 
 def local(
@@ -418,15 +473,16 @@
     w_gate, w_up, w_down, gain_final, w_reward,
 ):
     ids = jnp.arange(64, dtype=jnp.int32)
-    inverse = jnp.sum(ids[:, None] * (shard_order[:, None] == ids[None, :]).astype(jnp.int32), axis=0)
-    zs, xs, ys = inverse // 16, (inverse // 4) % 4, inverse % 4
-    pos = jnp.stack([ys * 16 + xs * 4 + zs, xs * 16 + ys * 4 + zs])
-    gains = jnp.stack([gain_attn, gain_ff, gain_final, w_reward])
-    wt = jnp.concatenate([w_out, w_down], axis=0).T
+    zs, xs, ys = ids // 16, (ids // 4) % 4, ids % 4
+    half = jnp.arange(2, dtype=jnp.int32)[:, None, None]
+    slot = jnp.where(half == 0, ys * 16 + xs * 4, xs * 16 + ys * 4) + zs
+    pos = jnp.sum(jnp.where(shard_order[None, None, :] == ids[None, :, None], slot, 0), axis=2)
     rows, normalized = layer(
-        pos, lengths, rel_bias, hidden_states, gains, w_query, w_key, w_value, w_gate, w_up, wt
+        pos, lengths, rel_bias.T, hidden_states,
+        gain_attn.reshape(1, D), gain_ff.reshape(1, D), gain_final.reshape(1, D), w_reward.reshape(1, D),
+        w_query, w_key, w_value, w_gate, w_up, w_out.T, w_down.T,
     )
-    return rows, normalized[0, :1]
+    return rows, normalized.reshape(1)
 
 
 def solution(mesh):

time: 198 us -> 192 us (0.970)
  other arithmetic: 4.17 us -> 0.78 us
  Pallas kernels: 187 us -> 185 us
    another operation x2 -> x0, other arithmetic: 1.99 us -> none  [the longest x1 1.4 us: local(): gains = jnp.stack([gain_attn, gain_ff, gain_final, w_reward])]
where the time goes in v4:
time: 192 us
  Pallas kernels  185 us (96%)
  between operations  3 us (2%)
  local copies, waits for them, and re-layouts  2.87 us (1%)
    pallas_call x1, Pallas kernels, layer(): pl.pallas_call(layer_kernel, out_shape=(jax.ShapeDtypeStruct((ROWS, D), F...  185 us

profile of v4, /device:TPU:1, one launch (start us, length us, event | category | flops | bytes accessed | tf_op | source)
XLA Modules:
  0.0 192.1 jit_solution(2478514110885664624)
XLA Ops:
  1.3 0.0 copy-start
  1.3 0.1 select_add_fusion
  1.4 0.6 copy-done
  2.0 0.7 select_reduce_fusion.refs_0_
  2.7 185.4 %layer.1 = (f32[128,2048]{1,0:T(8,128)}, f32[1,1]{1,0:T(1,128)}) custom-call(s32[2,64]{1,0:T(2,128)} %select_reduce_fusion.refs_0_, s32[1]{0:T(128)S(6)} %copy.19.refs_1_, f32[8,32]{1,0:T(8,128)} %bitcast.14, f32[128,2048]{1,0:T(8,128)} %refs_3_.1, f32[1,2048]{1,0:T(1,128)} %bitcast.10, f32[1,2048]{1,0:T(1,128)} %bitcast.11, f32[1,2048]{1,0:T(1,128)} %bitcast.12, ...), custom_call_target="tpu_custom_call" | custom-call | tf_op jit(solution)/shard_map/layer/pallas_call | solution.py:458
  188.1 2.3 %copy.20 = f32[128,2048]{1,0:T(8,128)} copy(f32[128,2048]{1,0:T(8,128)} %get-tuple-element.10) | data formatting | bytes 2097152
  (4 shorter events, 0.0 us)
Async XLA Ops:
  1.3 0.7 copy-start

commit v5 on v4

--- a/solution.py
+++ b/solution.py
@@ -287,7 +287,7 @@
     lax.fori_loop(2, 3, pair, 0)
     events((2, 4), (3, 3))
     lax.fori_loop(3, 4, pair, 0)
-    events((4, 1), (2, 5))
+    events((4, 1), (5, 1), (6, 1), (2, 5))
 
     rows_far, rows_own = pl.ds((1 - h) * 2, 2), pl.ds(h * 2, 2)
 
@@ -309,7 +309,7 @@
         lax.fori_loop(0, 4, lambda i, _: out_tile(rows_own, g, i), 0)
         to_sibling(0, g, wa, *xa)
         to_far(g, wa, r1a, s2a, r2a, ea_send, ea_recv)
-    events((5, 1), (6, 1), (4, 2), (3, 4), (5, 2), (6, 2), (4, 3), (5, 3))
+    events((4, 2), (5, 2), (6, 2), (3, 4), (4, 3), (5, 3))
     for g in range(GA):
         cols = slice(g * wa, (g + 1) * wa)
         mid[:, cols] = mid[:, cols] + total(g, wa, r1a, r2a, ea_recv)

time: 192 us -> 191 us (level)
  no operation moved by 1% of the time
where the time goes in v5:
time: 191 us
  Pallas kernels  184 us (96%)
  between operations  3 us (2%)
  local copies, waits for them, and re-layouts  2.87 us (2%)
    pallas_call x1, Pallas kernels, layer(): pl.pallas_call(layer_kernel, out_shape=(jax.ShapeDtypeStruct((ROWS, D), F...  184 us

profile of v5, /device:TPU:1, one launch (start us, length us, event | category | flops | bytes accessed | tf_op | source)
XLA Modules:
  0.0 190.7 jit_solution(8576750472428172610)
XLA Ops:
  1.3 0.0 copy-start
  1.3 0.1 select_add_fusion
  1.4 0.6 copy-done
  2.0 0.7 select_reduce_fusion.refs_0_
  2.7 184.0 %layer.1 = (f32[128,2048]{1,0:T(8,128)}, f32[1,1]{1,0:T(1,128)}) custom-call(s32[2,64]{1,0:T(2,128)} %select_reduce_fusion.refs_0_, s32[1]{0:T(128)S(6)} %copy.19.refs_1_, f32[8,32]{1,0:T(8,128)} %bitcast.14, f32[128,2048]{1,0:T(8,128)} %refs_3_.1, f32[1,2048]{1,0:T(1,128)} %bitcast.10, f32[1,2048]{1,0:T(1,128)} %bitcast.11, f32[1,2048]{1,0:T(1,128)} %bitcast.12, ...), custom_call_target="tpu_custom_call" | custom-call | tf_op jit(solution)/shard_map/layer/pallas_call | solution.py:458
  186.7 2.3 %copy.20 = f32[128,2048]{1,0:T(8,128)} copy(f32[128,2048]{1,0:T(8,128)} %get-tuple-element.10) | data formatting | bytes 2097152
  (4 shorter events, 0.0 us)
Async XLA Ops:
  1.3 0.7 copy-start

commit v6 on v5

--- a/solution.py
+++ b/solution.py
@@ -74,6 +74,10 @@
             return [big.at[:, slice(0, 768) if ch == 3 else slice(768, 1280)]]
         return [wdown.at[slice(0, 16) if ch == 5 else slice(16, 32), col * 640 : col * 640 + 640]]
 
+    barrier = pltpu.get_barrier_semaphore()
+    for k in (8, 7, 9, 6, 10, 5, 11, 4, 12, 3, 13, 2, 14, 1, 15):
+        pl.semaphore_signal(barrier, inc=1, device_id=line_peer(k), device_id_type=MESH)
+        pl.semaphore_signal(barrier, inc=1, device_id=plane_peer(k), device_id_type=MESH)
     for ch in range(NC):
         for col in (0, 1):
             at = 0
@@ -83,10 +87,6 @@
                 pltpu.make_async_copy(piece, here, loc_sem.at[col, ch]).start()
                 at += n
 
-    barrier = pltpu.get_barrier_semaphore()
-    for k in range(1, 16):
-        pl.semaphore_signal(barrier, inc=1, device_id=line_peer(k), device_id_type=MESH)
-        pl.semaphore_signal(barrier, inc=1, device_id=plane_peer(k), device_id_type=MESH)
     pl.semaphore_wait(barrier, 30)
 
     ring1, ring2 = (x, y), (y, x)

time: 191 us -> 191 us (level)
  no operation moved by 1% of the time
where the time goes in v6:
time: 191 us
  Pallas kernels  184 us (96%)
  between operations  3 us (2%)
  local copies, waits for them, and re-layouts  2.87 us (2%)
    pallas_call x1, Pallas kernels, layer(): pl.pallas_call(layer_kernel, out_shape=(jax.ShapeDtypeStruct((ROWS, D), F...  184 us

profile of v6, /device:TPU:1, one launch (start us, length us, event | category | flops | bytes accessed | tf_op | source)
XLA Modules:
  0.0 190.6 jit_solution(2150978545794997315)
XLA Ops:
  1.3 0.0 copy-start
  1.3 0.1 select_add_fusion
  1.4 0.6 copy-done
  2.0 0.7 select_reduce_fusion.refs_0_
  2.7 184.0 %layer.1 = (f32[128,2048]{1,0:T(8,128)}, f32[1,1]{1,0:T(1,128)}) custom-call(s32[2,64]{1,0:T(2,128)} %select_reduce_fusion.refs_0_, s32[1]{0:T(128)S(6)} %copy.19.refs_1_, f32[8,32]{1,0:T(8,128)} %bitcast.14, f32[128,2048]{1,0:T(8,128)} %refs_3_.1, f32[1,2048]{1,0:T(1,128)} %bitcast.10, f32[1,2048]{1,0:T(1,128)} %bitcast.11, f32[1,2048]{1,0:T(1,128)} %bitcast.12, ...), custom_call_target="tpu_custom_call" | custom-call | tf_op jit(solution)/shard_map/layer/pallas_call | solution.py:458
  186.7 2.3 %copy.20 = f32[128,2048]{1,0:T(8,128)} copy(f32[128,2048]{1,0:T(8,128)} %get-tuple-element.10) | data formatting | bytes 2097152
  (4 shorter events, 0.0 us)
Async XLA Ops:
  1.3 0.7 copy-start
